TPU v7x, 128 devices: a whole 4x4x4 slice. The times are simulated.
128 devices in a mesh: graph: 1, nodes: 128 (over z, y, x, core).
Axes of the slice: x: 4, y: 4, z: 4, core: 2. Of those that a mesh axis runs over, the one named last changes fastest.
Arguments:
- node_feats: bfloat16 [131072, 200], P(('graph', 'nodes'))
- a_int: bfloat16 [131072, 1024], P(('graph', 'nodes'))
- a_halo: bfloat16 [131072, 512], P(('graph', 'nodes'))
- send_idx: int32 [512, 128], P(('graph', 'nodes'))
- w_first: bfloat16 [200, 512], replicated
- w_second: bfloat16 [512, 107], replicated
- grad_out: bfloat16 [131072, 107], P(('graph', 'nodes'))
Outputs:
- output 1: float32 [200, 512], P('graph')
- output 2: float32 [512, 107], P('graph')
- output 3: float32 [131072, 200], P(('graph', 'nodes'))
All inputs are finite; a program needn't handle non-finite values.
Results may differ from a plain program's by a relative error of at most 0.00585534.
Values are sent between devices in bfloat16 or wider.
A program may use at most 1 GiB of HBM per device.

v0:
```python
import jax
import jax.numpy as jnp
from jax import lax
from jax.sharding import PartitionSpec as P


def link_offsets(num_links):
    return [(link // 2 + 1) * (1 - 2 * (link % 2)) for link in range(num_links)]


def shift_pairs(axis_size, offset):
    return [(source, (source + offset) % axis_size) for source in range(axis_size)]


def contract_rows(left_rows, right_rows):
    return lax.dot_general(left_rows, right_rows, (((0,), (0,)), ((), ())), preferred_element_type=jnp.float32)


def halo_rows(features, send_idx, axis_size):
    sent_rows = jnp.take(features, send_idx, axis=0)
    received = [lax.ppermute(sent_rows[link], "nodes", shift_pairs(axis_size, offset)) for link, offset in enumerate(link_offsets(send_idx.shape[0]))]
    return jnp.concatenate(received, axis=0)


def aggregate(a_int, a_halo, features, send_idx, axis_size):
    remote = halo_rows(features, send_idx, axis_size)
    return jnp.dot(a_int, features, preferred_element_type=jnp.float32) + jnp.dot(a_halo, remote, preferred_element_type=jnp.float32)


def aggregate_back(a_int, a_halo, grad_rows, send_idx, axis_size):
    num_slots = send_idx.shape[1]
    inner_sum = contract_rows(a_int, grad_rows)
    outward = contract_rows(a_halo, grad_rows).astype(jnp.bfloat16)
    received = [lax.ppermute(outward[link * num_slots:(link + 1) * num_slots], "nodes", shift_pairs(axis_size, -offset)) for link, offset in enumerate(link_offsets(send_idx.shape[0]))]
    returned = jnp.concatenate(received, axis=0).astype(jnp.float32)
    return inner_sum.at[send_idx.reshape(-1)].add(returned)


def solution(mesh):
    axis_size = mesh.shape["nodes"]
    row_spec = P(("graph", "nodes"), None)
    replicated = P(None, None)
    part_spec = P("graph", None)

    def device_step(node_feats, a_int, a_halo, send_idx, w_first, w_second, grad_out):
        z_first = aggregate(a_int, a_halo, node_feats, send_idx, axis_size).astype(jnp.bfloat16)
        hidden = jnp.maximum(jnp.dot(z_first, w_first, preferred_element_type=jnp.float32), 0.0).astype(jnp.bfloat16)
        z_second = aggregate(a_int, a_halo, hidden, send_idx, axis_size).astype(jnp.bfloat16)
        dw_second = lax.psum(contract_rows(z_second, grad_out), "nodes")
        dz_second = lax.dot_general(grad_out, w_second, (((1,), (1,)), ((), ())), preferred_element_type=jnp.float32).astype(jnp.bfloat16)
        d_hidden = aggregate_back(a_int, a_halo, dz_second, send_idx, axis_size)
        grad_pre = jnp.where(hidden > 0, d_hidden, 0.0).astype(jnp.bfloat16)
        dw_first = lax.psum(contract_rows(z_first, grad_pre), "nodes")
        dz_first = lax.dot_general(grad_pre, w_first, (((1,), (1,)), ((), ())), preferred_element_type=jnp.float32).astype(jnp.bfloat16)
        grad_feats = aggregate_back(a_int, a_halo, dz_first, send_idx, axis_size)
        return dw_first, dw_second, grad_feats

    return jax.shard_map(device_step, mesh=mesh, in_specs=(row_spec, row_spec, row_spec, row_spec, replicated, replicated, row_spec), out_specs=(part_spec, part_spec, row_spec), check_vma=False)
```

profile of v0, /device:TPU:1, one launch (start us, length us, event | category | flops | bytes accessed | tf_op | source)
XLA Modules:
  0.0 258.0 jit_solution(7693757200536265739)
XLA Ops:
  7.2 0.0 copy-start
  7.2 0.0 all-reduce.3.cloned.1.call-start
  7.2 0.8 fusion.26
  8.1 0.7 compare_and_fusion
  8.7 0.0 copy-start.8
  8.8 1.3 copy.10
  10.0 2.0 gather_fusion
  12.0 0.0 copy-start.2
  12.0 0.1 broadcast_select_fusion.1
  12.2 0.7 slice_bitcast_fusion.7
  12.8 9.2 %collective-permute-start.3 = (bf16[128,200]{1,0:T(8,128)(2,1)}, bf16[128,200]{1,0:T(8,128)(2,1)S(1)}, u32[]{:S(2)}, u32[]{:S(2)}) collective-permute-start(bf16[128,200]{1,0:T(8,128)(2,1)} %get-tuple-element.17), channel_id=1, source_target_pairs={{0,126},{1,127},{2,0},{3,1},{4,2},{5,3},{6,4},{7,5},{8,6},{9,7},{1... | collective-permute-start | bytes 153608 | tf_op jit(solution)/shard_map/ppermute | solution.py:21
  22.1 1.0 collective-permute-start.1
  23.0 0.8 collective-permute-start
  23.8 0.5 convolution_convert_fusion
  24.3 0.0 copy-start.4
  24.3 0.7 fusion.3
  25.0 0.8 fusion.31
  25.9 0.0 collective-permute-start.7
  25.9 0.8 fusion.33
  26.7 0.0 copy-start.12
  26.7 2.6 %convolution_bitcast_fusion = f32[1024,512]{0,1:T(8,128)} fusion(bf16[1024,512]{1,0:T(8,128)(2,1)S(1)} %convolution_convert_fusion, bf16[1024,1024]{1,0:T(8,128)(2,1)S(1)} %copy-done), kind=kOutput, calls=%fused_computation.7 | convolution fusion | flops 1073741824 | bytes 5242880 | tf_op jit(solution)/shard_map/dot_general | solution.py:16
  29.3 0.6 compare_select_fusion
  29.9 2.9 %copy.11 = f32[1024,512]{1,0:T(8,128)} copy(f32[1024,512]{0,1:T(8,128)} %convolution_bitcast_fusion) | data formatting | bytes 4194304 | tf_op jit(solution)/shard_map/dot_general | solution.py:16
  32.8 0.0 collective-permute-done.3
  32.8 12.4 %collective-permute-start.6 = (bf16[128,512]{0,1:T(8,128)(2,1)}, bf16[128,512]{0,1:T(8,128)(2,1)}, u32[]{:S(2)}, u32[]{:S(2)}) collective-permute-start(bf16[128,512]{0,1:T(8,128)(2,1)} %get-tuple-element.14), channel_id=1, source_target_pairs={{0,126},{1,127},{2,0},{3,1},{4,2},{5,3},{6,4},{7,5},{8,6},{9,7},{1... | collective-permute-start | bytes 393224 | tf_op jit(solution)/shard_map/ppermute | solution.py:34
  45.2 0.0 collective-permute-done.2
  45.2 0.0 collective-permute-done.1
  45.2 0.7 collective-permute-start.4
  46.0 0.0 collective-permute-done
  46.0 1.9 fusion.2
  47.9 0.5 maximum_convert_fusion
  48.4 2.6 %fusion.34 = f32[512,1024]{1,0:T(8,128)} fusion(bf16[1024,512]{1,0:T(8,128)(2,1)S(1)} %maximum_convert_fusion, bf16[1024,1024]{1,0:T(8,128)(2,1)S(1)} %copy-done), kind=kOutput, calls=%fused_computation.56 | convolution fusion | flops 1073741824 | bytes 5242880 | tf_op jit(solution)/shard_map/dot_general | solution.py:27
  51.0 2.8 %gather_fusion.1 = bf16[512,512]{1,0:T(8,128)(2,1)} fusion(bf16[1024,512]{1,0:T(8,128)(2,1)S(1)} %maximum_convert_fusion, s32[1024]{0:T(1024)} %copy-done.13), kind=kCustom, calls=%fused_computation.1 | custom fusion | bytes 1050624 | tf_op jit(solution)/shard_map/jit(_take)/gather | solution.py:20
  53.8 1.2 broadcast_select_fusion
  55.0 0.8 slice_bitcast_fusion.3
  55.8 7.3 %collective-permute-start.11 = (bf16[128,512]{1,0:T(8,128)(2,1)}, bf16[128,512]{1,0:T(8,128)(2,1)}, u32[]{:S(2)}, u32[]{:S(2)}) collective-permute-start(bf16[128,512]{1,0:T(8,128)(2,1)} %get-tuple-element.9), channel_id=1, source_target_pairs={{0,126},{1,127},{2,0},{3,1},{4,2},{5,3},{6,4},{7,5},{8,6},{9,7},{1... | collective-permute-start | bytes 393224 | tf_op jit(solution)/shard_map/ppermute | solution.py:21
  63.1 1.8 collective-permute-start.9
  64.9 0.0 collective-permute-start.8
  64.9 2.2 maximum_convert_fusion.1
  67.1 2.6 copy.12
  69.7 7.2 %scatter_fusion = f32[1024,512]{1,0:T(8,128)} fusion(f32[1024,512]{1,0:T(8,128)} %copy.11, s32[512]{0:T(512)} %bitcast.59, f32[512,512]{1,0:T(8,128)} %copy.12), kind=kCustom, calls=%fused_computation.2 | custom fusion | flops 262144 | bytes 3147776 | tf_op jit(solution)/shard_map/scatter-add | solution.py:36
  76.9 2.9 %fusion.30 = f32[200,512]{1,0:T(8,128)} fusion(bf16[1024,200]{0,1:T(8,128)(2,1)S(1)} %fusion.2, f32[1024,512]{1,0:T(8,128)} %scatter_fusion, bf16[1024,512]{1,0:T(8,128)(2,1)S(1)} %maximum_convert_fusion), kind=kOutput, calls=%fused_computation.52 | convolution fusion | flops 211812352 | bytes 3964928 | tf_op jit(solution)/shard_map/dot_general | solution.py:16
  79.8 0.5 convolution_convert_fusion.2
  80.3 0.7 copy-done.3
  81.0 0.4 fusion.4
  81.4 0.7 fusion.32
  82.1 0.0 collective-permute-start.15
  82.1 0.0 collective-permute-done.11
  82.1 12.3 %collective-permute-start.14 = (bf16[128,200]{0,1:T(8,128)(2,1)}, bf16[128,200]{0,1:T(8,128)(2,1)}, u32[]{:S(2)}, u32[]{:S(2)}) collective-permute-start(bf16[128,200]{0,1:T(8,128)(2,1)} %get-tuple-element.22), channel_id=1, source_target_pairs={{0,126},{1,127},{2,0},{3,1},{4,2},{5,3},{6,4},{7,5},{8,6},{9,7},{1... | collective-permute-start | bytes 153608 | tf_op jit(solution)/shard_map/ppermute | solution.py:34
  94.4 0.0 collective-permute-done.10
  94.4 0.7 collective-permute-start.12
  95.2 3.8 %fusion = f32[512,107]{0,1:T(8,128)} fusion(bf16[1024,107]{0,1:T(8,128)(2,1)} %param.13, f32[512,1024]{1,0:T(8,128)} %fusion.34, bf16[1024,512]{1,0:T(8,128)(2,1)} %param.9, bf16[128,512]{1,0:T(8,128)(2,1)} %collective-permute-done.11, bf16[128,512]{1,0:T(8,128)(2,1)} %collective-permute-done.10, bf16[128,512]{1,0:T(8,128)(2,1)} %collective-permute-done.9, ...), kind=kOutput, calls=%fused_computation.9 | convolution fusion | flops 652214272 | bytes 4108288 | tf_op jit(solution)/shard_map/dot_general | solution.py:16
  99.0 0.0 all-reduce.3.cloned.1.call-update
  99.0 1.5 convolution_bitcast_fusion.2
  100.5 1.5 copy.13
  102.0 0.0 collective-permute-done.14
  102.0 0.0 collective-permute-done.13
  102.1 0.9 maximum_convert_fusion.2
  103.0 1.0 copy.14
  104.0 4.3 %scatter_fusion.1 = f32[1024,200]{1,0:T(8,128)S(1)} fusion(f32[1024,200]{1,0:T(8,128)S(1)} %copy.13, s32[512]{0:T(512)} %bitcast.60, f32[512,200]{1,0:T(8,128)} %copy.14), kind=kCustom, calls=%fused_computation.3 | custom fusion | flops 102400 | bytes 1230848 | tf_op jit(solution)/shard_map/scatter-add | solution.py:36
  108.3 1.2 copy.15
  109.5 138.2 %all-reduce.3.cloned.1.call-done = (f32[200,512]{1,0:T(8,128)}, f32[512,107]{0,1:T(8,128)}) async-done(((f32[200,512]{1,0:T(8,128)}, f32[512,107]{0,1:T(8,128)}), (f32[200,512]{1,0:T(8,128)}, f32[512,107]{0,1:T(8,128)})) %all-reduce.3.cloned.1.call-update) | async-done | bytes 628752 | tf_op jit(solution)/shard_map/psum | solution.py:53
  247.7 1.8 copy.20
  249.5 1.6 copy.21
  (37 shorter events, 0.1 us)
Async XLA Ops:
  7.2 18.7 %copy-start = (bf16[1024,1024]{1,0:T(8,128)(2,1)S(1)}, bf16[1024,1024]{1,0:T(8,128)(2,1)}, u32[]{:S(2)}) copy-start(bf16[1024,1024]{1,0:T(8,128)(2,1)} %param.8) | copy-start | bytes 6291460
  7.2 240.6 %all-reduce.3.cloned.1.call-start = ((), (), s32[]{:S(2)}) async-start(), calls=%async_computation | async-start | bytes 1277952 | tf_op jit(solution)/shard_map/psum | solution.py:53
  8.7 4.1 %copy-start.14 = (pred[4,128]{1,0:T(4,128)(4,1)}, pred[4,128]{1,0:T(4,128)(4,1)S(1)}, u32[]{:S(2)}) copy-start(pred[4,128]{1,0:T(4,128)(4,1)S(1)} %compare_and_fusion) | copy-start | bytes 1540
  8.7 15.1 %copy-start.5 = (bf16[1024,107]{0,1:T(8,128)(2,1)S(1)}, bf16[1024,107]{0,1:T(8,128)(2,1)}, u32[]{:S(2)}) copy-start(bf16[1024,107]{0,1:T(8,128)(2,1)} %param.13) | copy-start | bytes 657412
  8.7 15.1 %copy-start.8 = (bf16[512,107]{0,1:T(8,128)(2,1)S(1)}, bf16[512,107]{0,1:T(8,128)(2,1)}, u32[]{:S(2)}) copy-start(bf16[512,107]{0,1:T(8,128)(2,1)} %param.12) | copy-start | bytes 328708
  10.0 2.8 %copy-start.13 = (s32[1024]{0:T(1024)}, s32[1024]{0:T(1024)S(1)}, u32[]{:S(2)}) copy-start(s32[1024]{0:T(1024)S(1)} %pad_clamp_fusion) | copy-start | bytes 12292
  12.0 12.3 %copy-start.2 = (bf16[1024,512]{1,0:T(8,128)(2,1)S(1)}, bf16[1024,512]{1,0:T(8,128)(2,1)}, u32[]{:S(2)}) copy-start(bf16[1024,512]{1,0:T(8,128)(2,1)} %param.9) | copy-start | bytes 3145732
  12.8 20.0 %collective-permute-start.3 = (bf16[128,200]{1,0:T(8,128)(2,1)}, bf16[128,200]{1,0:T(8,128)(2,1)S(1)}, u32[]{:S(2)}, u32[]{:S(2)}) collective-permute-start(bf16[128,200]{1,0:T(8,128)(2,1)} %get-tuple-element.17), channel_id=1, source_target_pairs={{0,126},{1,127},{2,0},{3,1},{4,2},{5,3},{6,4},{7,5},{8,6},{9,7},{1... | collective-permute-start | bytes 153608 | tf_op jit(solution)/shard_map/ppermute | solution.py:21
  22.0 23.2 %collective-permute-start.2 = (bf16[128,200]{1,0:T(8,128)(2,1)}, bf16[128,200]{1,0:T(8,128)(2,1)S(1)}, u32[]{:S(2)}, u32[]{:S(2)}) collective-permute-start(bf16[128,200]{1,0:T(8,128)(2,1)} %get-tuple-element.18), channel_id=1, source_target_pairs={{0,2},{1,3},{2,4},{3,5},{4,6},{5,7},{6,8},{7,9},{8,10},{9,11},{10,... | collective-permute-start | bytes 153608 | tf_op jit(solution)/shard_map/ppermute | solution.py:21
  22.1 23.2 %collective-permute-start.1 = (bf16[128,200]{1,0:T(8,128)(2,1)S(1)}, bf16[128,200]{1,0:T(8,128)(2,1)S(1)}, u32[]{:S(2)}, u32[]{:S(2)}) collective-permute-start(bf16[128,200]{1,0:T(8,128)(2,1)S(1)} %get-tuple-element.19), channel_id=1, source_target_pairs={{0,127},{1,0},{2,1},{3,2},{4,3},{5,4},{6,5},{7,6},{8,7},{9,8},{10,... | collective-permute-start | bytes 153608 | tf_op jit(solution)/shard_map/ppermute | solution.py:21
  23.0 23.0 %collective-permute-start = (bf16[128,200]{1,0:T(8,128)(2,1)S(1)}, bf16[128,200]{1,0:T(8,128)(2,1)}, u32[]{:S(2)}, u32[]{:S(2)}) collective-permute-start(bf16[128,200]{1,0:T(8,128)(2,1)S(1)} %get-tuple-element.16), channel_id=1, source_target_pairs={{0,1},{1,2},{2,3},{3,4},{4,5},{5,6},{6,7},{7,8},{8,9},{9,10},{10,1... | collective-permute-start | bytes 153608 | tf_op jit(solution)/shard_map/ppermute | solution.py:21
  24.3 1.6 copy-start.4
  25.9 37.2 %collective-permute-start.7 = (bf16[128,512]{0,1:T(8,128)(2,1)}, bf16[128,512]{0,1:T(8,128)(2,1)}, u32[]{:S(2)}, u32[]{:S(2)}) collective-permute-start(bf16[128,512]{0,1:T(8,128)(2,1)} %get-tuple-element.13), channel_id=1, source_target_pairs={{0,2},{1,3},{2,4},{3,5},{4,6},{5,7},{6,8},{7,9},{8,10},{9,11},{10,... | collective-permute-start | bytes 393224 | tf_op jit(solution)/shard_map/ppermute | solution.py:34
  26.7 2.6 %copy-start.12 = (s32[4,128]{1,0:T(4,128)S(1)}, s32[4,128]{1,0:T(4,128)}, u32[]{:S(2)}) copy-start(s32[4,128]{1,0:T(4,128)} %param.10) | copy-start | bytes 6148
  32.8 15.1 %copy-start.6 = (bf16[200,512]{1,0:T(8,128)(2,1)S(1)}, bf16[200,512]{1,0:T(8,128)(2,1)}, u32[]{:S(2)}) copy-start(bf16[200,512]{1,0:T(8,128)(2,1)} %param.11) | copy-start | bytes 614404
  32.8 13.2 %copy-start.9 = (bf16[128,200]{1,0:T(8,128)(2,1)}, bf16[128,200]{1,0:T(8,128)(2,1)S(1)}, u32[]{:S(2)}) copy-start(bf16[128,200]{1,0:T(8,128)(2,1)S(1)} %collective-permute-done.3) | copy-start | bytes 153604
  32.8 30.3 %collective-permute-start.6 = (bf16[128,512]{0,1:T(8,128)(2,1)}, bf16[128,512]{0,1:T(8,128)(2,1)}, u32[]{:S(2)}, u32[]{:S(2)}) collective-permute-start(bf16[128,512]{0,1:T(8,128)(2,1)} %get-tuple-element.14), channel_id=1, source_target_pairs={{0,126},{1,127},{2,0},{3,1},{4,2},{5,3},{6,4},{7,5},{8,6},{9,7},{1... | collective-permute-start | bytes 393224 | tf_op jit(solution)/shard_map/ppermute | solution.py:34
  45.2 0.8 copy-start.10
  45.2 19.7 %collective-permute-start.5 = (bf16[128,512]{0,1:T(8,128)(2,1)}, bf16[128,512]{0,1:T(8,128)(2,1)}, u32[]{:S(2)}, u32[]{:S(2)}) collective-permute-start(bf16[128,512]{0,1:T(8,128)(2,1)} %get-tuple-element.15), channel_id=1, source_target_pairs={{0,1},{1,2},{2,3},{3,4},{4,5},{5,6},{6,7},{7,8},{8,9},{9,10},{10,1... | collective-permute-start | bytes 393224 | tf_op jit(solution)/shard_map/ppermute | solution.py:34
  45.2 0.8 copy-start.11
  45.2 19.7 %collective-permute-start.4 = (bf16[128,512]{0,1:T(8,128)(2,1)}, bf16[128,512]{0,1:T(8,128)(2,1)}, u32[]{:S(2)}, u32[]{:S(2)}) collective-permute-start(bf16[128,512]{0,1:T(8,128)(2,1)} %get-tuple-element.12), channel_id=1, source_target_pairs={{0,127},{1,0},{2,1},{3,2},{4,3},{5,4},{6,5},{7,6},{8,7},{9,8},{10,... | collective-permute-start | bytes 393224 | tf_op jit(solution)/shard_map/ppermute | solution.py:34
  55.8 26.3 %collective-permute-start.11 = (bf16[128,512]{1,0:T(8,128)(2,1)}, bf16[128,512]{1,0:T(8,128)(2,1)}, u32[]{:S(2)}, u32[]{:S(2)}) collective-permute-start(bf16[128,512]{1,0:T(8,128)(2,1)} %get-tuple-element.9), channel_id=1, source_target_pairs={{0,126},{1,127},{2,0},{3,1},{4,2},{5,3},{6,4},{7,5},{8,6},{9,7},{1... | collective-permute-start | bytes 393224 | tf_op jit(solution)/shard_map/ppermute | solution.py:21
  63.1 31.3 %collective-permute-start.10 = (bf16[128,512]{1,0:T(8,128)(2,1)}, bf16[128,512]{1,0:T(8,128)(2,1)}, u32[]{:S(2)}, u32[]{:S(2)}) collective-permute-start(bf16[128,512]{1,0:T(8,128)(2,1)} %get-tuple-element.10), channel_id=1, source_target_pairs={{0,2},{1,3},{2,4},{3,5},{4,6},{5,7},{6,8},{7,9},{8,10},{9,11},{10,... | collective-permute-start | bytes 393224 | tf_op jit(solution)/shard_map/ppermute | solution.py:21
  63.1 31.3 %collective-permute-start.9 = (bf16[128,512]{1,0:T(8,128)(2,1)}, bf16[128,512]{1,0:T(8,128)(2,1)}, u32[]{:S(2)}, u32[]{:S(2)}) collective-permute-start(bf16[128,512]{1,0:T(8,128)(2,1)} %get-tuple-element.11), channel_id=1, source_target_pairs={{0,127},{1,0},{2,1},{3,2},{4,3},{5,4},{6,5},{7,6},{8,7},{9,8},{10,... | collective-permute-start | bytes 393224 | tf_op jit(solution)/shard_map/ppermute | solution.py:21
  64.9 30.3 %collective-permute-start.8 = (bf16[128,512]{1,0:T(8,128)(2,1)}, bf16[128,512]{1,0:T(8,128)(2,1)}, u32[]{:S(2)}, u32[]{:S(2)}) collective-permute-start(bf16[128,512]{1,0:T(8,128)(2,1)} %get-tuple-element.8), channel_id=1, source_target_pairs={{0,1},{1,2},{2,3},{3,4},{4,5},{5,6},{6,7},{7,8},{8,9},{9,10},{10,1... | collective-permute-start | bytes 393224 | tf_op jit(solution)/shard_map/ppermute | solution.py:21
  76.9 2.9 %copy-start.1 = (f32[1024,512]{1,0:T(8,128)S(1)}, f32[1024,512]{1,0:T(8,128)}, u32[]{:S(2)}) copy-start(f32[1024,512]{1,0:T(8,128)} %scatter_fusion) | copy-start | bytes 6291460
  76.9 2.9 %copy-start.7 = (bf16[200,512]{1,0:T(8,128)(2,1)S(1)}, bf16[200,512]{1,0:T(8,128)(2,1)}, u32[]{:S(2)}) copy-start(bf16[200,512]{1,0:T(8,128)(2,1)} %param.11) | copy-start | bytes 614404
  79.8 1.2 copy-start.3
  82.1 19.9 %collective-permute-start.15 = (bf16[128,200]{0,1:T(8,128)(2,1)}, bf16[128,200]{0,1:T(8,128)(2,1)}, u32[]{:S(2)}, u32[]{:S(2)}) collective-permute-start(bf16[128,200]{0,1:T(8,128)(2,1)} %get-tuple-element.21), channel_id=1, source_target_pairs={{0,2},{1,3},{2,4},{3,5},{4,6},{5,7},{6,8},{7,9},{8,10},{9,11},{10,... | collective-permute-start | bytes 153608 | tf_op jit(solution)/shard_map/ppermute | solution.py:34
  82.1 19.9 %collective-permute-start.14 = (bf16[128,200]{0,1:T(8,128)(2,1)}, bf16[128,200]{0,1:T(8,128)(2,1)}, u32[]{:S(2)}, u32[]{:S(2)}) collective-permute-start(bf16[128,200]{0,1:T(8,128)(2,1)} %get-tuple-element.22), channel_id=1, source_target_pairs={{0,126},{1,127},{2,0},{3,1},{4,2},{5,3},{6,4},{7,5},{8,6},{9,7},{1... | collective-permute-start | bytes 153608 | tf_op jit(solution)/shard_map/ppermute | solution.py:34
  94.4 7.6 %collective-permute-start.13 = (bf16[128,200]{0,1:T(8,128)(2,1)}, bf16[128,200]{0,1:T(8,128)(2,1)}, u32[]{:S(2)}, u32[]{:S(2)}) collective-permute-start(bf16[128,200]{0,1:T(8,128)(2,1)} %get-tuple-element.23), channel_id=1, source_target_pairs={{0,1},{1,2},{2,3},{3,4},{4,5},{5,6},{6,7},{7,8},{8,9},{9,10},{10,1... | collective-permute-start | bytes 153608 | tf_op jit(solution)/shard_map/ppermute | solution.py:34
  94.4 7.6 %collective-permute-start.12 = (bf16[128,200]{0,1:T(8,128)(2,1)}, bf16[128,200]{0,1:T(8,128)(2,1)}, u32[]{:S(2)}, u32[]{:S(2)}) collective-permute-start(bf16[128,200]{0,1:T(8,128)(2,1)} %get-tuple-element.20), channel_id=1, source_target_pairs={{0,127},{1,0},{2,1},{3,2},{4,3},{5,4},{6,5},{7,6},{8,7},{9,8},{10,... | collective-permute-start | bytes 153608 | tf_op jit(solution)/shard_map/ppermute | solution.py:34
Sparse Core Ops, SparseCore 0:
  99.2 148.5 all-reduce.2
where the time goes:
time: 259 us; the launch traced here: 258 us
  waiting for transfers between devices  138 us (53%)
  starting transfers between devices  46.4 us (18%)
  local copies, waits for them, and re-layouts  22.3 us (9%)
  matrix products  18.8 us (7%)
  other arithmetic  18 us (7%)
  between operations  14.3 us (6%)
    psum x1, waiting for transfers between devices, device_step(): dw_first = lax.psum(contract_rows(z_first, grad_pre), 'nodes')  138 us
    ppermute x8, starting transfers between devices, aggregate_back(): lax.ppermute(outward[link * num_slots:(link + 1) * num_slots], 'nodes', s...  26.2 us
    ppermute x8, starting transfers between devices, halo_rows(): lax.ppermute(sent_rows[link], 'nodes', shift_pairs(axis_size, offset))  20.1 us
    dot_general x6, matrix products, contract_rows(): lax.dot_general(left_rows, right_rows, (((0,), (0,)), ((), ())), preferre...  12 us
    scatter-add x2, other arithmetic, aggregate_back(): return inner_sum.at[send_idx.reshape(-1)].add(returned)  11.5 us
    unnamed x34, local copies, waits for them, and re-layouts  6.67 us
  transfers between devices with their start and end apart: 17, of which 1 were waited for; matrix products, arithmetic and copies ran while one was open for 19% of the time, Pallas kernels for 0%

commit v1 on v0

v1 whole, which is shorter than its diff:
```python
import functools

import jax
import jax.numpy as jnp
from jax import lax
from jax.experimental import pallas as pl
from jax.experimental.pallas import tpu as pltpu
from jax.sharding import PartitionSpec as P

BF = jnp.bfloat16
F32 = jnp.float32
OFFSETS = (1, -1, 2, -2)
SLOTS = 128
CHUNKS = 64
ANY = pl.BlockSpec(memory_space=pl.ANY)


def torus_dims(n):
    return {128: (4, 4, 4, 2), 16: (2, 2, 2, 2)}[n]


def dot(a, b):
    return jnp.dot(a, b, preferred_element_type=F32)


def dot_nt(a, b):
    return lax.dot_general(a, b, (((1,), (1,)), ((), ())), preferred_element_type=F32)


def blocks(total, block, body):
    if total <= block:
        body(pl.ds(0, total))
        return

    @pl.loop(0, total // block)
    def _(i):
        body(pl.ds(pl.multiple_of(i * block, block), block))


def kernel(n, x_hbm, aint_hbm, ahalo_hbm, idx_hbm, w0_hbm, w1_hbm, g_hbm, dw1_hbm, dw2_hbm, gf_hbm,
           x, aint, ahalo, idx, w0, w1, g, s, e1t, o1, r1, g0, h0, zpart, d1t, z0, h1, h1t, g1, hh1, z1part,
           w0t, gt, ft, e0t, o0, r0, gfacc, gfout, dw1out, dw2out,
           ar, res, rs1, rs2, load_sem, out_sem, halo_send, halo_recv, p1s, p1r, p2s, p2r, p3s, p3r, p4s, p4r):
    dims = torus_dims(n)
    nz, ny, nx, nc = dims
    strides = (ny * nx * nc, nx * nc, nc, 1)
    me = lax.axis_index("nodes")
    pos = [lax.rem(lax.div(me, st), d) for st, d in zip(strides, dims)]
    core = pos[3]

    def at(delta):
        return sum(lax.rem(pos[a] + delta[a], dims[a]) * strides[a] for a in range(4))

    near = set()
    for dz in range(nz):
        for dy in range(ny):
            for dx in range(nx):
                moved = (dz > 0) + (dy > 0) + (dx > 0)
                if 0 < moved < 3:
                    near.add((dz, dy, dx, 0))
                if moved <= 1:
                    near.add((dz, dy, dx, 1))
    near = sorted(near)
    partners = [lax.rem(me + o + n, n) for o in OFFSETS]

    barrier = pltpu.get_barrier_semaphore()
    for d in partners + [at(delta) for delta in near]:
        pl.semaphore_signal(barrier, inc=1, device_id={"nodes": d})

    loads = [pltpu.make_async_copy(src, dst, load_sem.at[i]) for i, (src, dst) in enumerate([
        (idx_hbm, idx), (x_hbm, x), (w1_hbm, w1), (g_hbm, g), (ahalo_hbm, ahalo), (aint_hbm, aint), (w0_hbm, w0)])]
    for load in loads:
        load.start()

    def halo_copies(which, src, dst, sign):
        return [pltpu.make_async_remote_copy(
            src_ref=src(k), dst_ref=dst(k), send_sem=halo_send.at[which, k], recv_sem=halo_recv.at[which, k],
            device_id={"nodes": lax.rem(me + sign * o + n, n)}) for k, o in enumerate(OFFSETS)]

    rows = lambda k: pl.ds(k * SLOTS, SLOTS)
    copy_h0 = halo_copies(0, lambda k: g0.at[rows(k)], lambda k: h0.at[rows(k)], 1)
    copy_d1 = halo_copies(1, lambda k: o1.at[k], lambda k: r1.at[k], -1)
    copy_h1 = halo_copies(2, lambda k: g1.at[rows(k)], lambda k: hh1.at[rows(k)], 1)
    copy_d0 = halo_copies(3, lambda k: o0.at[k], lambda k: r0.at[k], -1)

    nodes = x.shape[0]
    loads[0].wait()
    lane = lax.broadcasted_iota(jnp.int32, (SLOTS, SLOTS), 1)
    for k in range(4):
        col = jnp.broadcast_to(idx[k:k + 1, :], (SLOTS, SLOTS)).T
        for b in range(nodes // SLOTS):
            s[rows(k), b * SLOTS:(b + 1) * SLOTS] = jnp.where(col == lane + b * SLOTS, 1.0, 0.0).astype(BF)

    loads[1].wait()
    g0[...] = dot(s[...], x[...]).astype(BF)
    pl.semaphore_wait(barrier, len(partners) + len(near))
    for copy in copy_h0:
        copy.start()

    loads[2].wait()
    loads[3].wait()

    def make_e1(r):
        e1t[r] = dot_nt(w1[r], g[...]).astype(BF)
    blocks(w1.shape[0], 256, make_e1)
    loads[4].wait()

    def make_o1(r):
        out = dot(e1t[r], ahalo[...]).astype(BF)
        for k in range(4):
            o1[k, r] = out[:, k * SLOTS:(k + 1) * SLOTS]
    blocks(w1.shape[0], 256, make_o1)
    for copy in copy_d1:
        copy.start()

    loads[5].wait()
    loads[6].wait()

    def make_zpart(r):
        zpart[r] = dot(aint[r], x[...])
    blocks(nodes, 256, make_zpart)

    feats = x.shape[1]
    z0[:, 128:] = jnp.zeros((nodes, 128), BF)
    pad = jnp.zeros((256 - feats, w0.shape[1]), F32)
    w0t[...] = jnp.concatenate([w0[...].astype(F32), pad], axis=0).T.astype(BF)
    classes = g.shape[1]
    gt[...] = jnp.zeros(gt.shape, BF)
    gt[0:classes, :] = g[...].astype(F32).T.astype(BF)

    for copy in copy_h0:
        copy.wait_recv()

    def make_h1(r):
        z = (zpart[r] + dot(ahalo[r], h0[...])).astype(BF)
        z0[r, 0:feats] = z
        h1[r] = jnp.maximum(dot(z, w0[...]), 0.0).astype(BF)
    blocks(nodes, 256, make_h1)

    def make_g1(r):
        g1[r] = dot(s[r], h1[...]).astype(BF)
    blocks(4 * SLOTS, 256, make_g1)
    for copy in copy_h1:
        copy.start()

    def make_d1(r):
        d1t[r] = dot(e1t[r], aint[...])
    blocks(w1.shape[0], 256, make_d1)

    def make_h1t(r):
        h1t[r] = jnp.maximum(dot_nt(w0t[r], z0[...]), 0.0).astype(BF)
    blocks(w1.shape[0], 256, make_h1t)

    for copy in copy_d1:
        copy.wait_recv()

    def make_ft(r):
        back = jnp.concatenate([r1[k, r] for k in range(4)], axis=1)
        d1 = d1t[r] + dot(back, s[...])
        ft[r] = jnp.where(h1t[r] > 0, d1, 0.0).astype(BF)
    blocks(w1.shape[0], 256, make_ft)

    def line_of(b):
        return (1, 2, 0)[b]

    def group_size(b):
        return dims[line_of(b)] * nc

    def group_dev(b, q):
        a = line_of(b)
        return me - pos[a] * strides[a] - core + lax.div(q, nc) * strides[a] + lax.rem(q, nc)

    def plane_axes(b):
        return [a for a in range(3) if a != line_of(b)]

    def plane_size(b):
        u, v = plane_axes(b)
        return dims[u] * dims[v]

    def plane_dev(b, p):
        u, v = plane_axes(b)
        return (me - pos[u] * strides[u] - pos[v] * strides[v] + lax.div(p, dims[v]) * strides[u] + lax.rem(p, dims[v]) * strides[v])

    class Sum:
        def __init__(self, b):
            self.b = b
            self.gs, self.ps = group_size(b), plane_size(b)
            self.piece = CHUNKS // self.gs
            self.owners = min(self.piece, self.ps)
            self.part = self.piece // self.owners
            self.q = pos[line_of(b)] * nc + core
            u, v = plane_axes(b)
            self.p = pos[u] * dims[v] + pos[v]

        def copy1(self, d):
            b = self.b
            to = lax.rem(self.q + d, self.gs)
            return pltpu.make_async_remote_copy(
                src_ref=ar.at[b, pl.ds(to * self.piece, self.piece)], dst_ref=rs1.at[b, d - 1],
                send_sem=p1s.at[b, d - 1], recv_sem=p1r.at[b, d - 1], device_id={"nodes": group_dev(b, to)})

        def copy2(self, d):
            b = self.b
            to = lax.rem(self.p + d, self.ps)
            first = self.q * self.piece + lax.rem(to, self.owners) * self.part
            return to, pltpu.make_async_remote_copy(
                src_ref=ar.at[b, pl.ds(first, self.part)], dst_ref=rs2.at[b, d - 1],
                send_sem=p2s.at[b, d - 1], recv_sem=p2r.at[b, d - 1], device_id={"nodes": plane_dev(b, to)})

        def copy3(self, d):
            b = self.b
            to = lax.rem(self.p + d, self.ps)
            mine = pl.ds(self.q * self.piece + lax.rem(self.p, self.owners) * self.part, self.part)
            return pltpu.make_async_remote_copy(
                src_ref=res.at[b, mine], dst_ref=res.at[b, mine],
                send_sem=p3s.at[b, d - 1], recv_sem=p3r.at[b, d - 1], device_id={"nodes": plane_dev(b, to)})

        def copy4(self, d):
            b = self.b
            to = lax.rem(self.q + d, self.gs)
            mine = pl.ds(self.q * self.piece, self.piece)
            return pltpu.make_async_remote_copy(
                src_ref=res.at[b, mine], dst_ref=res.at[b, mine],
                send_sem=p4s.at[b, d - 1], recv_sem=p4r.at[b, d - 1], device_id={"nodes": group_dev(b, to)})

        def start1(self):
            for d in range(1, self.gs):
                self.copy1(d).start()

        def step2(self):
            for d in range(1, self.gs):
                self.copy1(d).wait()
            mine = pl.ds(self.q * self.piece, self.piece)
            ar[self.b, mine] = ar[self.b, mine] + jnp.sum(rs1[self.b], axis=0)
            for d in range(1, self.ps):
                to, copy = self.copy2(d)

                @pl.when(to < self.owners)
                def _():
                    copy.start()

        def step3(self):
            for d in range(1, self.ps):
                to, copy = self.copy2(d)

                @pl.when(to < self.owners)
                def _():
                    copy.wait_send()

            @pl.when(self.p < self.owners)
            def _():
                for d in range(1, self.ps):
                    self.copy2(d)[1].wait_recv()
                mine = pl.ds(self.q * self.piece + lax.rem(self.p, self.owners) * self.part, self.part)
                res[self.b, mine] = ar[self.b, mine] + jnp.sum(rs2[self.b], axis=0)
                for d in range(1, self.ps):
                    self.copy3(d).start()

        def step4(self):
            for d in range(1, self.ps):
                source = lax.rem(self.p - d + self.ps, self.ps)

                @pl.when(source < self.owners)
                def _():
                    self.copy3(d).wait_recv()

            @pl.when(self.p < self.owners)
            def _():
                for d in range(1, self.ps):
                    self.copy3(d).wait_send()
            for d in range(1, self.gs):
                self.copy4(d).start()

        def finish(self):
            for d in range(1, self.gs):
                self.copy4(d).wait()

    sums = [Sum(b) for b in range(3)]

    def make_dw1(r):
        part = dot(ft[r], z0[...])
        chunk = pl.ds(lax.div(r.start, 8) if not isinstance(r.start, int) else r.start // 8, r.size // 8)
        ar[0, chunk] = part[:, 0:128].reshape(r.size // 8, 8, 128)
        ar[1, chunk] = part[:, 128:256].reshape(r.size // 8, 8, 128)
    blocks(w1.shape[0], 256, make_dw1)
    sums[0].start1()
    sums[1].start1()

    e0t[...] = dot(w0[...], ft[...]).astype(BF)
    out0 = dot(e0t[...], ahalo[...]).astype(BF)
    for k in range(4):
        o0[k] = out0[:, k * SLOTS:(k + 1) * SLOTS]
    for copy in copy_d0:
        copy.start()

    def make_z1part(r):
        z1part[r] = dot(aint[r], h1[...])
    blocks(nodes, 256, make_z1part)

    for copy in copy_h1:
        copy.wait_recv()

    def make_z1(r):
        h1[r] = (z1part[r] + dot(ahalo[r], hh1[...])).astype(BF)
    blocks(nodes, 256, make_z1)
    dw2t = dot(gt[...], h1[...])
    for b in range(4):
        ar[2, b * 16:(b + 1) * 16] = dw2t[:, b * 128:(b + 1) * 128].reshape(16, 8, 128)
    sums[2].start1()

    sums[0].step2()
    sums[1].step2()
    gfacc[0:feats, :] = dot(e0t[...], aint[...])
    sums[2].step2()
    for copy in copy_d0:
        copy.wait_recv()
    back0 = jnp.concatenate([r0[k] for k in range(4)], axis=1)
    gfacc[0:feats, :] = gfacc[0:feats, :] + dot(back0, s[...])
    sums[0].step3()
    sums[1].step3()
    gfacc[feats:, :] = jnp.zeros((256 - feats, nodes), F32)
    gfout[...] = gfacc[...].T[:, 0:feats]
    out_gf = pltpu.make_async_copy(gfout, gf_hbm, out_sem.at[0])
    out_gf.start()
    sums[2].step3()
    sums[0].step4()
    sums[1].step4()
    sums[2].step4()
    sums[0].finish()
    sums[1].finish()
    dw1out[0:128, :] = res[0].reshape(512, 128).T
    dw1out[128:feats, :] = res[1].reshape(512, 128).T[0:feats - 128, :]
    out_dw1 = pltpu.make_async_copy(dw1out, dw1_hbm, out_sem.at[1])
    out_dw1.start()
    sums[2].finish()
    for b in range(4):
        dw2out[b * 128:(b + 1) * 128, :] = res[2, b * 16:(b + 1) * 16].reshape(128, 128).T[:, 0:classes]
    out_dw2 = pltpu.make_async_copy(dw2out, dw2_hbm, out_sem.at[2])
    out_dw2.start()
    for copy in copy_h0 + copy_d1 + copy_h1 + copy_d0:
        copy.wait_send()
    out_gf.wait()
    out_dw1.wait()
    out_dw2.wait()


def solution(mesh):
    n = mesh.shape["nodes"]
    nz, ny, nx, nc = torus_dims(n)
    group = nx * nc
    plane = nx * ny
    row_spec = P(("graph", "nodes"), None)
    replicated = P(None, None)
    part_spec = P("graph", None)

    def device_step(node_feats, a_int, a_halo, send_idx, w_first, w_second, grad_out):
        nodes, feats = node_feats.shape
        hidden, classes = w_second.shape
        slots = a_halo.shape[1]
        piece = CHUNKS // group
        part = piece // min(piece, plane)
        v = pltpu.VMEM
        dma = pltpu.SemaphoreType.DMA
        return pl.pallas_call(
            functools.partial(kernel, n),
            out_shape=(jax.ShapeDtypeStruct((feats, hidden), F32), jax.ShapeDtypeStruct((hidden, classes), F32),
                       jax.ShapeDtypeStruct((nodes, feats), F32)),
            in_specs=[ANY] * 7,
            out_specs=[ANY] * 3,
            scratch_shapes=[
                v((nodes, feats), BF), v((nodes, nodes), BF), v((nodes, slots), BF), v((4, SLOTS), jnp.int32),
                v((feats, hidden), BF), v((hidden, classes), BF), v((nodes, classes), BF),
                v((slots, nodes), BF),
                v((hidden, nodes), BF),
                v((4, hidden, SLOTS), BF),
                v((4, hidden, SLOTS), BF),
                v((slots, feats), BF),
                v((slots, feats), BF),
                v((nodes, feats), F32),
                v((hidden, nodes), F32),
                v((nodes, 256), BF),
                v((nodes, hidden), BF),
                v((hidden, nodes), BF),
                v((slots, hidden), BF),
                v((slots, hidden), BF),
                v((nodes, hidden), F32),
                v((hidden, 256), BF),
                v((128, nodes), BF),
                v((hidden, nodes), BF),
                v((feats, nodes), BF),
                v((4, feats, SLOTS), BF),
                v((4, feats, SLOTS), BF),
                v((256, nodes), F32),
                v((nodes, feats), F32),
                v((feats, hidden), F32),
                v((hidden, classes), F32),
                v((3, CHUNKS, 8, 128), F32),
                v((3, CHUNKS, 8, 128), F32),
                v((3, group - 1, piece, 8, 128), F32),
                v((3, plane - 1, part, 8, 128), F32),
                dma((7,)), dma((3,)), dma((4, 4)), dma((4, 4)),
                dma((3, group - 1)), dma((3, group - 1)), dma((3, plane - 1)), dma((3, plane - 1)),
                dma((3, plane - 1)), dma((3, plane - 1)), dma((3, group - 1)), dma((3, group - 1)),
            ],
            compiler_params=pltpu.CompilerParams(collective_id=0, has_side_effects=True),
        )(node_feats, a_int, a_halo, send_idx, w_first, w_second, grad_out)

    return jax.shard_map(device_step, mesh=mesh, in_specs=(row_spec, row_spec, row_spec, row_spec, replicated, replicated, row_spec), out_specs=(part_spec, part_spec, row_spec), check_vma=False)
```

time: 259 us -> 64.3 us (0.25)
  waiting for transfers between devices: 138 us -> 0 us
  Pallas kernels: 0 us -> 52.9 us
  starting transfers between devices: 46.4 us -> 0 us
  matrix products: 18.8 us -> 0 us
  other arithmetic: 18 us -> 0 us
  between operations: 14.3 us -> 0.65 us
  local copies, waits for them, and re-layouts: 22.3 us -> 10.5 us
    psum x1 -> x0, waiting for transfers between devices: 138 us -> none  [device_step(): dw_first = lax.psum(contract_rows(z_first, grad_pre), 'nodes')]
    pallas_call x0 -> x1, Pallas kernels: none -> 52.9 us  [device_step(): pl.pallas_call(functools.partial(kernel, n), out_shape=(jax.ShapeDtypeStr...]
    ppermute x16 -> x0, starting transfers between devices: 46.3 us -> none  [the longest x8 26.2 us: aggregate_back(): lax.ppermute(outward[link * num_slots:(link + 1) * num_slots], 'nodes', s...]
    dot_general x12 -> x0, matrix products: 18.8 us -> none  [the longest x6 12 us: contract_rows(): lax.dot_general(left_rows, right_rows, (((0,), (0,)), ((), ())), preferre...]
    scatter-add x2 -> x0, other arithmetic: 11.5 us -> none  [aggregate_back(): return inner_sum.at[send_idx.reshape(-1)].add(returned)]
    gather x2 -> x0, local copies, waits for them, and re-layouts: 4.71 us -> none  [halo_rows(): sent_rows = jnp.take(features, send_idx, axis=0)]
    dot_general x2 -> x0, local copies, waits for them, and re-layouts: 4.35 us -> none  [contract_rows(): lax.dot_general(left_rows, right_rows, (((0,), (0,)), ((), ())), preferre...]
    pallas_call x0 -> x2, local copies, waits for them, and re-layouts: none -> 4.27 us  [device_step(): pl.pallas_call(functools.partial(kernel, n), out_shape=(jax.ShapeDtypeStr...]
  transfers between devices with their start and end apart: 17 -> 0, of which waited for: 1 -> 0; matrix products, arithmetic and copies ran while one was open for 19% -> 0% of each run, Pallas kernels for 0% -> 0%
where the time goes in v1:
time: 64.3 us; the launch traced here: 64 us
  Pallas kernels  52.9 us (82%)
  local copies, waits for them, and re-layouts  10.5 us (16%)
  between operations  0.65 us (1%)
    pallas_call x1, Pallas kernels, device_step(): pl.pallas_call(functools.partial(kernel, n), out_shape=(jax.ShapeDtypeStr...  52.9 us
    unnamed x6, local copies, waits for them, and re-layouts  6.21 us
    pallas_call x2, local copies, waits for them, and re-layouts, device_step(): pl.pallas_call(functools.partial(kernel, n), out_shape=(jax.ShapeDtypeStr...  4.27 us

profile of v1, /device:TPU:1, one launch (start us, length us, event | category | flops | bytes accessed | tf_op | source)
XLA Modules:
  0.0 64.0 jit_solution(9874928989883873068)
XLA Ops:
  0.6 1.7 %copy.11.w1_hbm = bf16[512,107]{1,0:T(8,128)(2,1)} copy(bf16[512,107]{0,1:T(8,128)(2,1)} %param.12) | data formatting | bytes 219136 | tf_op args[5]
  2.3 1.8 %copy.12.g_hbm = bf16[1024,107]{1,0:T(8,128)(2,1)} copy(bf16[1024,107]{0,1:T(8,128)(2,1)} %param.13) | data formatting | bytes 438272 | tf_op args[6]
  4.1 2.0 %copy.10.x_hbm = bf16[1024,200]{1,0:T(8,128)(2,1)} copy(bf16[1024,200]{0,1:T(8,128)(2,1)} %param.7) | data formatting | bytes 819200 | tf_op args[0]
  6.1 52.9 %shard_map.94 = (f32[200,512]{1,0:T(8,128)}, f32[512,107]{1,0:T(8,128)}, f32[1024,200]{1,0:T(8,128)}) custom-call(bf16[1024,200]{1,0:T(8,128)(2,1)} %copy.10.x_hbm, bf16[1024,1024]{1,0:T(8,128)(2,1)} %aint_hbm.1, bf16[1024,512]{1,0:T(8,128)(2,1)} %ahalo_hbm.1, s32[4,128]{1,0:T(4,128)} %idx_hbm.1, bf16[200,512]{1,0:T(8,128)(2,1)} %w0_hbm.1, ...), custom_call_target="tpu_custom_call" | custom-call | tf_op jit(solution)/shard_map/pallas_call | solution.py:364
  59.0 0.0 copy-start
  59.0 1.8 %copy.13 = f32[512,107]{0,1:T(8,128)} copy(f32[512,107]{1,0:T(8,128)} %get-tuple-element.4) | data formatting | bytes 438272 | tf_op jit(solution)/shard_map/pallas_call | solution.py:364
  60.8 2.4 %copy.14 = f32[1024,200]{0,1:T(8,128)} copy(f32[1024,200]{1,0:T(8,128)} %get-tuple-element.5) | data formatting | bytes 1638400 | tf_op jit(solution)/shard_map/pallas_call | solution.py:364
  63.3 0.0 copy-done
  63.3 0.8 %copy.16 = f32[200,512]{1,0:T(8,128)} copy(f32[200,512]{1,0:T(8,128)S(1)} %copy-done) | data formatting | bytes 819200
Async XLA Ops:
  59.0 4.3 %copy-start = (f32[200,512]{1,0:T(8,128)S(1)}, f32[200,512]{1,0:T(8,128)}, u32[]{:S(2)}) copy-start(f32[200,512]{1,0:T(8,128)} %get-tuple-element.9) | copy-start | bytes 1228804

commit v2 on v1

v2 whole, which is shorter than its diff:
```python
import functools

import jax
import jax.numpy as jnp
from jax import lax
from jax.experimental import pallas as pl
from jax.experimental.pallas import tpu as pltpu
from jax.sharding import PartitionSpec as P

BF = jnp.bfloat16
F32 = jnp.float32
OFFSETS = (1, -1, 2, -2)
SLOTS = 128
CHUNKS = 56
USED = (56, 48, 56)
ANY = pl.BlockSpec(memory_space=pl.ANY)


def torus_dims(n):
    return {128: (4, 4, 4, 2), 16: (2, 2, 2, 2)}[n]


def dot(a, b):
    return jnp.dot(a, b, preferred_element_type=F32)


def dot_nt(a, b):
    return lax.dot_general(a, b, (((1,), (1,)), ((), ())), preferred_element_type=F32)


def kernel(n, xt_hbm, aint_hbm, ahalo_hbm, idx_hbm, w0_hbm, w1t_hbm, gt_hbm, dw1_hbm, dw2t_hbm, gft_hbm,
           xt, aint, ahalo, idx, w0, w1t, gt, st, s, e1t, o1, r1, g0, h0, zpart, d1t, z0t, h1t, g1, hh1, z1part, z1t,
           w0t, w1, gtp, ft, e0t, o0, r0, gft, dw1out, dw2out,
           ar, res, rs1, rs2, load_sem, out_sem, halo_send, halo_recv, p1s, p1r, p2s, p2r, p3s, p3r, p4s, p4r):
    dims = torus_dims(n)
    nz, ny, nx, nc = dims
    strides = (ny * nx * nc, nx * nc, nc, 1)
    me = lax.axis_index("nodes")
    pos = [lax.rem(lax.div(me, st_), d) for st_, d in zip(strides, dims)]
    core = pos[3]
    feats, nodes = xt.shape
    classes, hidden = w1t.shape

    def at(delta):
        return sum(lax.rem(pos[a] + delta[a], dims[a]) * strides[a] for a in range(4))

    near = set()
    for dz in range(nz):
        for dy in range(ny):
            for dx in range(nx):
                moved = (dz > 0) + (dy > 0) + (dx > 0)
                if 0 < moved < 3:
                    near.add((dz, dy, dx, 0))
                if moved <= 1:
                    near.add((dz, dy, dx, 1))
    near = sorted(near)
    partners = [lax.rem(me + o + n, n) for o in OFFSETS]

    barrier = pltpu.get_barrier_semaphore()
    for d in partners + [at(delta) for delta in near]:
        pl.semaphore_signal(barrier, inc=1, device_id={"nodes": d})

    loads = [pltpu.make_async_copy(src, dst, load_sem.at[i]) for i, (src, dst) in enumerate([
        (idx_hbm, idx), (xt_hbm, xt), (w1t_hbm, w1t), (gt_hbm, gt), (ahalo_hbm, ahalo), (aint_hbm, aint), (w0_hbm, w0)])]
    for load in loads:
        load.start()

    def halo_copies(which, src, dst, sign):
        return [pltpu.make_async_remote_copy(
            src_ref=src(k), dst_ref=dst(k), send_sem=halo_send.at[which, k], recv_sem=halo_recv.at[which, k],
            device_id={"nodes": lax.rem(me + sign * o + n, n)}) for k, o in enumerate(OFFSETS)]

    copy_h0 = halo_copies(0, lambda k: g0.at[k], lambda k: h0.at[k], 1)
    copy_d1 = halo_copies(1, lambda k: o1.at[k], lambda k: r1.at[k], -1)
    copy_h1 = halo_copies(2, lambda k: g1.at[k], lambda k: hh1.at[k], 1)
    copy_d0 = halo_copies(3, lambda k: o0.at[k], lambda k: r0.at[k], -1)

    def put(ref, value):
        for k in range(4):
            ref[k] = value[:, k * SLOTS:(k + 1) * SLOTS].astype(BF)

    def take(ref):
        return jnp.concatenate([ref[k] for k in range(4)], axis=1)

    loads[0].wait()
    sub = lax.broadcasted_iota(jnp.int32, (nodes, SLOTS), 0)
    for k in range(4):
        row = jnp.broadcast_to(idx[k:k + 1, :], (nodes, SLOTS))
        st[:, k * SLOTS:(k + 1) * SLOTS] = jnp.where(row == sub, 1.0, 0.0).astype(BF)

    loads[1].wait()
    put(g0, dot(xt[...], st[...]))
    pl.semaphore_wait(barrier, len(partners) + len(near))
    for copy in copy_h0:
        copy.start()

    loads[2].wait()
    loads[3].wait()
    w1[...] = jnp.concatenate([w1t[...].astype(F32), jnp.zeros((128 - classes, hidden), F32)], axis=0).T.astype(BF)
    gtp[...] = jnp.concatenate([gt[...].astype(F32), jnp.zeros((128 - classes, nodes), F32)], axis=0).astype(BF)
    e1t[...] = dot(w1[...], gtp[...]).astype(BF)
    loads[4].wait()
    put(o1, dot(e1t[...], ahalo[...]))
    for copy in copy_d1:
        copy.start()

    loads[5].wait()
    loads[6].wait()
    zpart[...] = dot_nt(xt[...], aint[...])
    w0t[...] = w0[...].astype(F32).T.astype(BF)
    lane = lax.broadcasted_iota(jnp.int32, (SLOTS, SLOTS), 1)
    for k in range(4):
        col = jnp.broadcast_to(idx[k:k + 1, :], (SLOTS, SLOTS)).T
        for b in range(nodes // SLOTS):
            s[k * SLOTS:(k + 1) * SLOTS, b * SLOTS:(b + 1) * SLOTS] = jnp.where(col == lane + b * SLOTS, 1.0, 0.0).astype(BF)

    for copy in copy_h0:
        copy.wait_recv()
    z0t[...] = (zpart[...] + dot_nt(take(h0), ahalo[...])).astype(BF)
    h1t[...] = jnp.maximum(dot(w0t[...], z0t[...]), 0.0).astype(BF)
    put(g1, dot(h1t[...], st[...]))
    for copy in copy_h1:
        copy.start()

    d1t[...] = dot(e1t[...], aint[...])

    for copy in copy_d1:
        copy.wait_recv()
    d1 = d1t[...] + dot(take(r1), s[...])
    ft[...] = jnp.where(h1t[...] > 0, d1, 0.0).astype(BF)

    def line_of(b):
        return (1, 2, 0)[b]

    def group_size(b):
        return dims[line_of(b)] * nc

    def group_dev(b, q):
        a = line_of(b)
        return me - pos[a] * strides[a] - core + lax.div(q, nc) * strides[a] + lax.rem(q, nc)

    def plane_axes(b):
        return [a for a in range(3) if a != line_of(b)]

    def plane_size(b):
        u, v = plane_axes(b)
        return dims[u] * dims[v]

    def plane_dev(b, p):
        u, v = plane_axes(b)
        return (me - pos[u] * strides[u] - pos[v] * strides[v] + lax.div(p, dims[v]) * strides[u] + lax.rem(p, dims[v]) * strides[v])

    class Sum:
        def __init__(self, b):
            self.b = b
            self.gs, self.ps = group_size(b), plane_size(b)
            self.piece, self.owners = shares(b, self.gs, self.ps)
            self.part = self.piece // self.owners
            self.q = pos[line_of(b)] * nc + core
            u, v = plane_axes(b)
            self.p = pos[u] * dims[v] + pos[v]

        def copy1(self, d):
            b = self.b
            to = lax.rem(self.q + d, self.gs)
            return pltpu.make_async_remote_copy(
                src_ref=ar.at[b, pl.ds(to * self.piece, self.piece)], dst_ref=rs1.at[b, d - 1, pl.ds(0, self.piece)],
                send_sem=p1s.at[b, d - 1], recv_sem=p1r.at[b, d - 1], device_id={"nodes": group_dev(b, to)})

        def copy2(self, d):
            b = self.b
            to = lax.rem(self.p + d, self.ps)
            first = self.q * self.piece + lax.rem(to, self.owners) * self.part
            return to, pltpu.make_async_remote_copy(
                src_ref=ar.at[b, pl.ds(first, self.part)], dst_ref=rs2.at[b, d - 1, pl.ds(0, self.part)],
                send_sem=p2s.at[b, d - 1], recv_sem=p2r.at[b, d - 1], device_id={"nodes": plane_dev(b, to)})

        def copy3(self, d):
            b = self.b
            to = lax.rem(self.p + d, self.ps)
            mine = pl.ds(self.q * self.piece + lax.rem(self.p, self.owners) * self.part, self.part)
            return pltpu.make_async_remote_copy(
                src_ref=res.at[b, mine], dst_ref=res.at[b, mine],
                send_sem=p3s.at[b, d - 1], recv_sem=p3r.at[b, d - 1], device_id={"nodes": plane_dev(b, to)})

        def copy4(self, d):
            b = self.b
            to = lax.rem(self.q + d, self.gs)
            mine = pl.ds(self.q * self.piece, self.piece)
            return pltpu.make_async_remote_copy(
                src_ref=res.at[b, mine], dst_ref=res.at[b, mine],
                send_sem=p4s.at[b, d - 1], recv_sem=p4r.at[b, d - 1], device_id={"nodes": group_dev(b, to)})

        def start1(self):
            for d in range(1, self.gs):
                self.copy1(d).start()

        def step2(self):
            for d in range(1, self.gs):
                self.copy1(d).wait()
            mine = pl.ds(self.q * self.piece, self.piece)
            ar[self.b, mine] = ar[self.b, mine] + jnp.sum(rs1[self.b, :, 0:self.piece], axis=0)
            for d in range(1, self.ps):
                to, copy = self.copy2(d)

                @pl.when(to < self.owners)
                def _():
                    copy.start()

        def step3(self):
            for d in range(1, self.ps):
                to, copy = self.copy2(d)

                @pl.when(to < self.owners)
                def _():
                    copy.wait_send()

            @pl.when(self.p < self.owners)
            def _():
                for d in range(1, self.ps):
                    self.copy2(d)[1].wait_recv()
                mine = pl.ds(self.q * self.piece + lax.rem(self.p, self.owners) * self.part, self.part)
                res[self.b, mine] = ar[self.b, mine] + jnp.sum(rs2[self.b, :, 0:self.part], axis=0)
                for d in range(1, self.ps):
                    self.copy3(d).start()

        def step4(self):
            for d in range(1, self.ps):
                source = lax.rem(self.p - d + self.ps, self.ps)

                @pl.when(source < self.owners)
                def _():
                    self.copy3(d).wait_recv()

            @pl.when(self.p < self.owners)
            def _():
                for d in range(1, self.ps):
                    self.copy3(d).wait_send()
            for d in range(1, self.gs):
                self.copy4(d).start()

        def finish(self):
            for d in range(1, self.gs):
                self.copy4(d).wait()

    sums = [Sum(b) for b in range(3)]

    def chunks(value, groups):
        return value.reshape(groups, 8, 128)

    dw1 = dot_nt(z0t[...], ft[...])
    for k in range(4):
        lanes = slice(k * 128, (k + 1) * 128)
        ar[0, k * 14:(k + 1) * 14] = chunks(dw1[0:112, lanes], 14)
        ar[1, k * 11:(k + 1) * 11] = chunks(dw1[112:200, lanes], 11)
    ar[1, 44:48] = jnp.zeros((4, 8, 128), F32)
    sums[0].start1()
    sums[1].start1()

    e0t[...] = dot(w0[...], ft[...]).astype(BF)
    put(o0, dot(e0t[...], ahalo[...]))
    for copy in copy_d0:
        copy.start()

    z1part[...] = dot_nt(h1t[...], aint[...])

    for copy in copy_h1:
        copy.wait_recv()
    z1t[...] = (z1part[...] + dot_nt(take(hh1), ahalo[...])).astype(BF)
    dw2t = dot_nt(gtp[...], z1t[...])
    for k in range(4):
        ar[2, k * 14:(k + 1) * 14] = chunks(dw2t[0:112, k * 128:(k + 1) * 128], 14)
    sums[2].start1()

    sums[0].step2()
    sums[1].step2()
    gft[...] = dot(e0t[...], aint[...])
    sums[2].step2()
    for copy in copy_d0:
        copy.wait_recv()
    gft[...] = gft[...] + dot(take(r0), s[...])
    out_gf = pltpu.make_async_copy(gft, gft_hbm, out_sem.at[0])
    out_gf.start()
    sums[0].step3()
    sums[1].step3()
    sums[2].step3()
    sums[0].step4()
    sums[1].step4()
    sums[2].step4()
    sums[0].finish()
    sums[1].finish()
    for k in range(4):
        lanes = slice(k * 128, (k + 1) * 128)
        dw1out[0:112, lanes] = res[0, k * 14:(k + 1) * 14].reshape(112, 128)
        dw1out[112:200, lanes] = res[1, k * 11:(k + 1) * 11].reshape(88, 128)
    out_dw1 = pltpu.make_async_copy(dw1out, dw1_hbm, out_sem.at[1])
    out_dw1.start()
    sums[2].finish()
    for k in range(4):
        dw2out[:, k * 128:(k + 1) * 128] = res[2, k * 14:(k + 1) * 14].reshape(112, 128)[0:classes]
    out_dw2 = pltpu.make_async_copy(dw2out, dw2t_hbm, out_sem.at[2])
    out_dw2.start()
    for copy in copy_h0 + copy_d1 + copy_h1 + copy_d0:
        copy.wait_send()
    out_gf.wait()
    out_dw1.wait()
    out_dw2.wait()


def shares(b, group, plane):
    piece = USED[b] // group
    return piece, max(d for d in range(1, plane + 1) if piece % d == 0)


def solution(mesh):
    n = mesh.shape["nodes"]
    nz, ny, nx, nc = torus_dims(n)
    group = nx * nc
    plane = nx * ny
    row_spec = P(("graph", "nodes"), None)
    replicated = P(None, None)
    part_spec = P("graph", None)

    def device_step(node_feats, a_int, a_halo, send_idx, w_first, w_second, grad_out):
        nodes, feats = node_feats.shape
        hidden, classes = w_second.shape
        slots = a_halo.shape[1]
        piece = CHUNKS // group
        part = max(shares(b, group, plane)[0] // shares(b, group, plane)[1] for b in range(3))
        v = pltpu.VMEM
        dma = pltpu.SemaphoreType.DMA
        dw1, dw2t, gft = pl.pallas_call(
            functools.partial(kernel, n),
            out_shape=(jax.ShapeDtypeStruct((feats, hidden), F32), jax.ShapeDtypeStruct((classes, hidden), F32),
                       jax.ShapeDtypeStruct((feats, nodes), F32)),
            in_specs=[ANY] * 7,
            out_specs=[ANY] * 3,
            scratch_shapes=[
                v((feats, nodes), BF),
                v((nodes, nodes), BF),
                v((nodes, slots), BF),
                v((4, SLOTS), jnp.int32),
                v((feats, hidden), BF),
                v((classes, hidden), BF),
                v((classes, nodes), BF),
                v((nodes, slots), BF),
                v((slots, nodes), BF),
                v((hidden, nodes), BF),
                v((4, hidden, SLOTS), BF),
                v((4, hidden, SLOTS), BF),
                v((4, feats, SLOTS), BF),
                v((4, feats, SLOTS), BF),
                v((feats, nodes), F32),
                v((hidden, nodes), F32),
                v((feats, nodes), BF),
                v((hidden, nodes), BF),
                v((4, hidden, SLOTS), BF),
                v((4, hidden, SLOTS), BF),
                v((hidden, nodes), F32),
                v((hidden, nodes), BF),
                v((hidden, feats), BF),
                v((hidden, 128), BF),
                v((128, nodes), BF),
                v((hidden, nodes), BF),
                v((feats, nodes), BF),
                v((4, feats, SLOTS), BF),
                v((4, feats, SLOTS), BF),
                v((feats, nodes), F32),
                v((feats, hidden), F32),
                v((classes, hidden), F32),
                v((3, CHUNKS, 8, 128), F32),
                v((3, CHUNKS, 8, 128), F32),
                v((3, group - 1, piece, 8, 128), F32),
                v((3, plane - 1, part, 8, 128), F32),
                dma((7,)), dma((3,)), dma((4, 4)), dma((4, 4)),
                dma((3, group - 1)), dma((3, group - 1)), dma((3, plane - 1)), dma((3, plane - 1)),
                dma((3, plane - 1)), dma((3, plane - 1)), dma((3, group - 1)), dma((3, group - 1)),
            ],
            compiler_params=pltpu.CompilerParams(collective_id=0, has_side_effects=True),
        )(node_feats.T, a_int, a_halo, send_idx, w_first, w_second.T, grad_out.T)
        return dw1, dw2t.T, gft.T

    return jax.shard_map(device_step, mesh=mesh, in_specs=(row_spec, row_spec, row_spec, row_spec, replicated, replicated, row_spec), out_specs=(part_spec, part_spec, row_spec), check_vma=False)
```

time: 64.3 us -> 55.9 us (0.87)
  local copies, waits for them, and re-layouts: 10.5 us -> 5.54 us
  Pallas kernels: 52.9 us -> 49.5 us
    pallas_call x2 -> x0, local copies, waits for them, and re-layouts: 4.27 us -> none  [device_step(): pl.pallas_call(functools.partial(kernel, n), out_shape=(jax.ShapeDtypeStr...]
    pallas_call x1, Pallas kernels: 52.9 us -> 49.5 us  [device_step(): pl.pallas_call(functools.partial(kernel, n), out_shape=(jax.ShapeDtypeStr...]
    unnamed x6 -> x3, local copies, waits for them, and re-layouts: 6.21 us -> 5.54 us
where the time goes in v2:
time: 55.9 us; the launch traced here: 55.6 us
  Pallas kernels  49.5 us (89%)
  local copies, waits for them, and re-layouts  5.54 us (10%)
  between operations  0.64 us (1%)
    pallas_call x1, Pallas kernels, device_step(): pl.pallas_call(functools.partial(kernel, n), out_shape=(jax.ShapeDtypeStr...  49.5 us
    unnamed x3, local copies, waits for them, and re-layouts  5.54 us

profile of v2, /device:TPU:1, one launch (start us, length us, event | category | flops | bytes accessed | tf_op | source)
XLA Modules:
  0.0 55.6 jit_solution(11138462662193471272)
XLA Ops:
  0.6 49.5 %shard_map.94 = (f32[200,512]{1,0:T(8,128)}, f32[107,512]{1,0:T(8,128)}, f32[200,1024]{1,0:T(8,128)}) custom-call(bf16[200,1024]{1,0:T(8,128)(2,1)} %bitcast.6, bf16[1024,1024]{1,0:T(8,128)(2,1)} %aint_hbm.1, bf16[1024,512]{1,0:T(8,128)(2,1)} %ahalo_hbm.1, s32[4,128]{1,0:T(4,128)} %idx_hbm.1, bf16[200,512]{1,0:T(8,128)(2,1)} %w0_hbm.1, ...), custom_call_target="tpu_custom_call" | custom-call | tf_op jit(solution)/shard_map/pallas_call | solution.py:332
  50.1 1.8 %copy.13 = f32[200,512]{1,0:T(8,128)} copy(f32[200,512]{1,0:T(8,128)} %get-tuple-element.12) | data formatting | bytes 819200
  51.9 1.6 %copy.14 = f32[512,107]{0,1:T(8,128)} copy(f32[512,107]{0,1:T(8,128)} %bitcast.7) | data formatting | bytes 438272
  53.5 2.1 %copy.15 = f32[1024,200]{0,1:T(8,128)} copy(f32[1024,200]{0,1:T(8,128)} %bitcast.5) | data formatting | bytes 1638400

commit v3 on v0

v3 whole, which is shorter than its diff:
```python
import functools

import jax
import jax.numpy as jnp
from jax import lax
from jax.experimental import pallas as pl
from jax.experimental.pallas import tpu as pltpu
from jax.sharding import PartitionSpec as P

BF = jnp.bfloat16
F32 = jnp.float32
OFFSETS = (1, -1, 2, -2)
SLOTS = 128
ANY = pl.BlockSpec(memory_space=pl.ANY)
VMEM = pl.BlockSpec(memory_space=pltpu.VMEM)
STAGES = (
    (("rs", "c"), ("rs", "zyx"), ("ag", "zyx"), ("ag", "c")),
    (("rs", "zyc"), ("bc", "x"), ("ag", "zyc")),
)
AXES = "zyxc"


def torus_dims(n):
    return {128: (4, 4, 4, 2), 16: (2, 2, 2, 2)}[n]


def dot(a, b):
    return jnp.dot(a, b, preferred_element_type=F32)


def dot_nt(a, b):
    return lax.dot_general(a, b, (((1,), (1,)), ((), ())), preferred_element_type=F32)


def plan(dims, stages, count):
    out, stack = [], []
    for kind, axes in stages:
        size = 1
        for a in axes:
            size *= dims[AXES.index(a)]
        if kind == "rs":
            piece = next(p for p in range(-(-count // size), count + 1) if count % p == 0)
            owners = count // piece
            out.append((kind, axes, size, owners, piece, (size - 1) * piece))
            stack.append((count, owners))
            count = piece
        elif kind == "bc":
            out.append((kind, axes, size, size, count, size * count))
        else:
            whole, owners = stack.pop()
            out.append((kind, axes, size, owners, count, 0))
            count = whole
    return out


def wait_bytes(ref, sem):
    pltpu.make_async_copy(ref, ref, sem).wait()


def when(condition, body):
    if condition is None:
        body()
    else:
        pl.when(condition)(body)


def both(a, b):
    if a is None or b is None:
        return b if a is None else a
    return jnp.logical_and(a, b)


class Sum:
    def __init__(self, me, pos, dims, strides, stages, count, ar, res, rb, send_sem, recv_sem):
        self.me, self.pos, self.dims, self.strides = me, pos, dims, strides
        self.ar, self.res, self.rb, self.send_sem, self.recv_sem = ar, res, rb, send_sem, recv_sem
        self.plan = plan(dims, stages, count)
        self.drains = []
        self.steps = self.run(count)

    def group(self, axes):
        ids = [AXES.index(a) for a in axes]
        p, base = 0, self.me
        for a in ids:
            p = p * self.dims[a] + self.pos[a]
            base = base - self.pos[a] * self.strides[a]

        def device(q):
            out = base
            for a in reversed(ids):
                out = out + lax.rem(q, self.dims[a]) * self.strides[a]
                q = lax.div(q, self.dims[a])
            return out
        return p, device

    def each(self, size, body):
        if size <= 8:
            for d in range(1, size):
                body(d)
        else:
            pl.loop(1, size)(body)

    def step(self):
        next(self.steps, None)

    def run(self, count):
        ar, res, rb = self.ar, self.res, self.rb
        first, active, offset, stack = 0, None, 0, []
        for i, (kind, axes, size, owners, piece, slots) in enumerate(self.plan):
            p, device = self.group(axes)
            send, recv = self.send_sem.at[i], self.recv_sem.at[i]
            to_of = lambda d: lax.rem(p + d, size)
            if kind == "rs":
                full = owners == size

                def start(d):
                    to = to_of(d)
                    copy = pltpu.make_async_remote_copy(
                        src_ref=ar.at[pl.ds(first + to * piece, piece)], dst_ref=rb.at[pl.ds(offset + (d - 1) * piece, piece)],
                        send_sem=send, recv_sem=recv, device_id={"nodes": device(to)})
                    when(None if full else to < owners, copy.start)
                when(active, lambda: self.each(size, start))
                yield
                mine = both(active, None if full else p < owners)
                new = first + p * piece
                got = pl.ds(offset, slots)

                def collect():
                    wait_bytes(rb.at[got], recv)
                    total = ar[pl.ds(new, piece)] + jnp.sum(rb[got].reshape(size - 1, piece, 8, 128), axis=0)
                    ar[pl.ds(new, piece)] = total
                    res[pl.ds(new, piece)] = total
                when(mine, collect)
                if full:
                    self.drains.append((active, send, (size - 1) * piece))
                else:
                    self.drains.append((mine, send, (owners - 1) * piece))
                    self.drains.append((both(active, p >= owners), send, owners * piece))
                stack.append((first, active, p, full))
                first, active = new, mine
                offset += slots
            elif kind == "bc":
                mine = pl.ds(first, piece)

                def start(d):
                    to = to_of(d)
                    pltpu.make_async_remote_copy(
                        src_ref=ar.at[mine], dst_ref=rb.at[pl.ds(offset + p * piece, piece)],
                        send_sem=send, recv_sem=recv, device_id={"nodes": device(to)}).start()

                def spread():
                    self.each(size, start)
                    rb[pl.ds(offset + p * piece, piece)] = ar[mine]
                when(active, spread)
                yield

                def collect():
                    wait_bytes(rb.at[pl.ds(offset, slots - piece)], recv)
                    res[mine] = jnp.sum(rb[pl.ds(offset, slots)].reshape(size, piece, 8, 128), axis=0)
                when(active, collect)
                self.drains.append((active, send, (size - 1) * piece))
                offset += slots
            else:
                mine = pl.ds(first, piece)

                def start(d):
                    pltpu.make_async_remote_copy(
                        src_ref=res.at[mine], dst_ref=res.at[mine],
                        send_sem=send, recv_sem=recv, device_id={"nodes": device(to_of(d))}).start()
                when(active, lambda: self.each(size, start))
                yield
                self.drains.append((active, send, (size - 1) * piece))
                first, active, p, full = stack.pop()
                if full:
                    when(active, lambda: wait_bytes(res.at[pl.ds(0, (size - 1) * piece)], recv))
                else:
                    when(both(active, p < owners), lambda: wait_bytes(res.at[pl.ds(0, (owners - 1) * piece)], recv))
                    when(both(active, p >= owners), lambda: wait_bytes(res.at[pl.ds(0, owners * piece)], recv))

    def drain(self):
        for condition, sem, slots in self.drains:
            when(condition, lambda: wait_bytes(self.rb.at[pl.ds(0, slots)], sem))


def kernel(n, xt_hbm, aint_hbm, ahalo_hbm, idx_hbm, w0_hbm, w1t_hbm, gt_hbm, dw1_ref, dw2t_ref, gft,
           xt, aint, ahalo, idx, w0, w1t, gt, st, s, e1t, o1, r1, g0, h0, zpart, d1t, z0t, h1t, g1, zh, z1part, z1t,
           w0t, w1, gtp, ft, e0t, o0, r0, ar1, res1, rb1, ar2, res2, rb2,
           load_sem, halo_send, halo_recv, send1, recv1, send2, recv2):
    dims = torus_dims(n)
    strides = tuple(dims[i + 1] * dims[i + 2] * dims[i + 3] if i == 0 else (dims[2] * dims[3], dims[3], 1)[i - 1] for i in range(4))
    me = lax.axis_index("nodes")
    pos = [lax.rem(lax.div(me, stride), d) for stride, d in zip(strides, dims)]
    feats, nodes = xt.shape
    classes, hidden = w1t.shape

    barrier = pltpu.get_barrier_semaphore()

    @pl.loop(1, n)
    def _(i):
        pl.semaphore_signal(barrier, inc=1, device_id={"nodes": lax.rem(me + i, n)})

    loads = [pltpu.make_async_copy(src, dst, load_sem.at[i]) for i, (src, dst) in enumerate([
        (idx_hbm, idx), (xt_hbm, xt), (w1t_hbm, w1t), (gt_hbm, gt), (ahalo_hbm, ahalo), (aint_hbm, aint), (w0_hbm, w0)])]
    for load in loads:
        load.start()

    class Halo:
        def __init__(self, which, src, dst, sign):
            self.src, self.dst = src, dst
            self.send, self.recv = halo_send.at[which], halo_recv.at[which]
            self.sign = sign

        def start(self):
            for k, o in enumerate(OFFSETS):
                pltpu.make_async_remote_copy(
                    src_ref=self.src.at[k], dst_ref=self.dst.at[k], send_sem=self.send, recv_sem=self.recv,
                    device_id={"nodes": lax.rem(me + self.sign * o + n, n)}).start()

        def wait_recv(self):
            wait_bytes(self.dst, self.recv)

        def wait_send(self):
            wait_bytes(self.src, self.send)

    halo_x = Halo(0, g0, h0, 1)
    halo_d1 = Halo(1, o1, r1, -1)
    halo_z = Halo(2, g1, zh, 1)
    halo_d0 = Halo(3, o0, r0, -1)
    sum1 = Sum(me, pos, dims, strides, STAGES[0], ar1.shape[0], ar1, res1, rb1, send1, recv1)
    sum2 = Sum(me, pos, dims, strides, STAGES[1], ar2.shape[0], ar2, res2, rb2, send2, recv2)

    def put(ref, value):
        for k in range(4):
            ref[k] = value[:, k * SLOTS:(k + 1) * SLOTS].astype(BF)

    def take(ref):
        return jnp.concatenate([ref[k] for k in range(4)], axis=1)

    loads[0].wait()
    sub = lax.broadcasted_iota(jnp.int32, (nodes, SLOTS), 0)
    for k in range(4):
        row = jnp.broadcast_to(idx[k:k + 1, :], (nodes, SLOTS))
        st[:, k * SLOTS:(k + 1) * SLOTS] = jnp.where(row == sub, 1.0, 0.0).astype(BF)

    loads[1].wait()
    put(g0, dot(xt[...], st[...]))
    loads[2].wait()
    loads[3].wait()
    w1[...] = jnp.concatenate([w1t[...].astype(F32), jnp.zeros((128 - classes, hidden), F32)], axis=0).T.astype(BF)
    gtp[...] = jnp.concatenate([gt[...].astype(F32), jnp.zeros((128 - classes, nodes), F32)], axis=0).astype(BF)
    e1t[...] = dot(w1[...], gtp[...]).astype(BF)
    loads[4].wait()
    put(o1, dot(e1t[...], ahalo[...]))

    pl.semaphore_wait(barrier, n - 1)
    halo_x.start()

    loads[5].wait()
    loads[6].wait()
    zpart[...] = dot_nt(xt[...], aint[...])
    halo_d1.start()
    w0t[...] = w0[...].astype(F32).T.astype(BF)
    lane = lax.broadcasted_iota(jnp.int32, (SLOTS, SLOTS), 1)
    for k in range(4):
        col = jnp.broadcast_to(idx[k:k + 1, :], (SLOTS, SLOTS)).T
        for b in range(nodes // SLOTS):
            s[k * SLOTS:(k + 1) * SLOTS, b * SLOTS:(b + 1) * SLOTS] = jnp.where(col == lane + b * SLOTS, 1.0, 0.0).astype(BF)
    d1t[...] = dot(e1t[...], aint[...])

    def hidden_of(zt):
        return jnp.maximum(dot(w0t[...], zt), 0.0).astype(BF)

    halo_x.wait_recv()
    z0t[...] = (zpart[...] + dot_nt(take(h0), ahalo[...])).astype(BF)
    put(g1, dot(z0t[...], st[...]))
    halo_z.start()
    h1t[...] = hidden_of(z0t[...])
    z1part[...] = dot_nt(h1t[...], aint[...])

    halo_d1.wait_recv()
    d1 = d1t[...] + dot(take(r1), s[...])
    ft[...] = jnp.where(h1t[...] > 0, d1, 0.0).astype(BF)

    def to_chunks(ref, value):
        groups = value.shape[0] // 8
        for k in range(hidden // 128):
            ref[k * groups:(k + 1) * groups] = value[:, k * 128:(k + 1) * 128].reshape(groups, 8, 128)

    def from_chunks(out_ref, ref, rows):
        groups = ref.shape[0] // (hidden // 128)
        for k in range(hidden // 128):
            out_ref[:, k * 128:(k + 1) * 128] = ref[k * groups:(k + 1) * groups].reshape(groups * 8, 128)[0:rows]

    to_chunks(ar1, dot_nt(z0t[...], ft[...]))
    sum1.step()
    e0t[...] = dot(w0[...], ft[...]).astype(BF)
    put(o0, dot(e0t[...], ahalo[...]))
    halo_d0.start()

    halo_z.wait_recv()
    z1t[...] = (z1part[...] + dot_nt(hidden_of(take(zh)), ahalo[...])).astype(BF)
    padded = -(-classes // 8) * 8
    to_chunks(ar2, dot_nt(gtp[...], z1t[...])[0:padded])
    sum2.step()

    sum1.step()
    gft[...] = dot(e0t[...], aint[...])
    sum2.step()
    sum1.step()
    sum2.step()
    halo_d0.wait_recv()
    gft[...] = gft[...] + dot(take(r0), s[...])
    for _ in range(3):
        sum1.step()
    from_chunks(dw1_ref, res1, feats)
    for _ in range(3):
        sum2.step()
    from_chunks(dw2t_ref, res2, classes)
    for halo in (halo_x, halo_d1, halo_z, halo_d0):
        halo.wait_send()
    sum1.drain()
    sum2.drain()


def write_out(a, b, c, x, y, z, sem):
    copies = [pltpu.make_async_copy(src, dst, sem.at[i]) for i, (src, dst) in enumerate([(a, x), (b, y), (c, z)])]
    for copy in copies:
        copy.start()
    for copy in copies:
        copy.wait()


def solution(mesh):
    n = mesh.shape["nodes"]
    dims = torus_dims(n)
    row_spec = P(("graph", "nodes"), None)
    replicated = P(None, None)
    part_spec = P("graph", None)

    def device_step(node_feats, a_int, a_halo, send_idx, w_first, w_second, grad_out):
        nodes, feats = node_feats.shape
        hidden, classes = w_second.shape
        slots = a_halo.shape[1]
        v = pltpu.VMEM
        dma = pltpu.SemaphoreType.DMA
        counts = (feats // 8 * (hidden // 128), -(-classes // 8) * (hidden // 128))
        sums = []
        for stages, count in zip(STAGES, counts):
            sums += [v((count, 8, 128), F32), v((count, 8, 128), F32), v((sum(p[5] for p in plan(dims, stages, count)), 8, 128), F32)]
        outs = pl.pallas_call(
            functools.partial(kernel, n),
            out_shape=(v((feats, hidden), F32), v((classes, hidden), F32), v((feats, nodes), F32)),
            in_specs=[ANY] * 7,
            out_specs=[VMEM] * 3,
            scratch_shapes=[
                v((feats, nodes), BF),
                v((nodes, nodes), BF),
                v((nodes, slots), BF),
                v((4, SLOTS), jnp.int32),
                v((feats, hidden), BF),
                v((classes, hidden), BF),
                v((classes, nodes), BF),
                v((nodes, slots), BF),
                v((slots, nodes), BF),
                v((hidden, nodes), BF),
                v((4, hidden, SLOTS), BF),
                v((4, hidden, SLOTS), BF),
                v((4, feats, SLOTS), BF),
                v((4, feats, SLOTS), BF),
                v((feats, nodes), F32),
                v((hidden, nodes), F32),
                v((feats, nodes), BF),
                v((hidden, nodes), BF),
                v((4, feats, SLOTS), BF),
                v((4, feats, SLOTS), BF),
                v((hidden, nodes), F32),
                v((hidden, nodes), BF),
                v((hidden, feats), BF),
                v((hidden, 128), BF),
                v((128, nodes), BF),
                v((hidden, nodes), BF),
                v((feats, nodes), BF),
                v((4, feats, SLOTS), BF),
                v((4, feats, SLOTS), BF),
                *sums,
                dma((7,)), dma((4,)), dma((4,)),
                dma((len(STAGES[0]),)), dma((len(STAGES[0]),)), dma((len(STAGES[1]),)), dma((len(STAGES[1]),)),
            ],
            compiler_params=pltpu.CompilerParams(collective_id=0, has_side_effects=True, vmem_limit_bytes=40 << 20),
        )(*[pltpu.with_memory_space_constraint(a, pltpu.HBM) for a in
            (node_feats.T, a_int, a_halo, send_idx, w_first, w_second.T, grad_out.T)])
        dw1, dw2t, gft = pl.pallas_call(
            write_out,
            out_shape=tuple(jax.ShapeDtypeStruct(o.shape, F32) for o in outs),
            in_specs=[VMEM] * 3,
            out_specs=[ANY] * 3,
            scratch_shapes=[dma((3,))],
            compiler_params=pltpu.CompilerParams(vmem_limit_bytes=1 << 20),
        )(*outs)
        return dw1, dw2t.T, gft.T

    return jax.shard_map(device_step, mesh=mesh, in_specs=(row_spec, row_spec, row_spec, row_spec, replicated, replicated, row_spec), out_specs=(part_spec, part_spec, row_spec), check_vma=False)
```

time: 259 us -> 42.9 us (0.17)
  waiting for transfers between devices: 138 us -> 0 us
  starting transfers between devices: 46.4 us -> 0 us
  Pallas kernels: 0 us -> 42.2 us
  local copies, waits for them, and re-layouts: 22.3 us -> 0 us
  matrix products: 18.8 us -> 0 us
  other arithmetic: 18 us -> 0 us
  between operations: 14.3 us -> 0.64 us
    psum x1 -> x0, waiting for transfers between devices: 138 us -> none  [device_step(): dw_first = lax.psum(contract_rows(z_first, grad_pre), 'nodes')]
    ppermute x16 -> x0, starting transfers between devices: 46.3 us -> none  [the longest x8 26.2 us: aggregate_back(): lax.ppermute(outward[link * num_slots:(link + 1) * num_slots], 'nodes', s...]
    pallas_call x0 -> x2, Pallas kernels: none -> 42.2 us  [the longest x1 41 us: device_step(): pl.pallas_call(functools.partial(kernel, n), out_shape=(v((feats, hidden)...]
    dot_general x12 -> x0, matrix products: 18.8 us -> none  [the longest x6 12 us: contract_rows(): lax.dot_general(left_rows, right_rows, (((0,), (0,)), ((), ())), preferre...]
    scatter-add x2 -> x0, other arithmetic: 11.5 us -> none  [aggregate_back(): return inner_sum.at[send_idx.reshape(-1)].add(returned)]
    unnamed x34 -> x0, local copies, waits for them, and re-layouts: 6.67 us -> none
    gather x2 -> x0, local copies, waits for them, and re-layouts: 4.71 us -> none  [halo_rows(): sent_rows = jnp.take(features, send_idx, axis=0)]
    dot_general x2 -> x0, local copies, waits for them, and re-layouts: 4.35 us -> none  [contract_rows(): lax.dot_general(left_rows, right_rows, (((0,), (0,)), ((), ())), preferre...]
  transfers between devices with their start and end apart: 17 -> 0, of which waited for: 1 -> 0; matrix products, arithmetic and copies ran while one was open for 19% -> 0% of each run, Pallas kernels for 0% -> 0%
where the time goes in v3:
time: 42.9 us; the launch traced here: 42.8 us
  Pallas kernels  42.2 us (98%)
  between operations  0.64 us (1%)
    pallas_call x1, Pallas kernels, device_step(): pl.pallas_call(functools.partial(kernel, n), out_shape=(v((feats, hidden)...  41 us
    pallas_call x1, Pallas kernels, device_step(): pl.pallas_call(write_out, out_shape=tuple((jax.ShapeDtypeStruct(o.shape,...  1.13 us

profile of v3, /device:TPU:1, one launch (start us, length us, event | category | flops | bytes accessed | tf_op | source)
XLA Modules:
  0.0 42.8 jit_solution(2054971004383653449)
XLA Ops:
  0.6 41.0 %shard_map.94 = (f32[200,512]{1,0:T(8,128)S(1)}, f32[107,512]{1,0:T(8,128)S(1)}, f32[200,1024]{1,0:T(8,128)S(1)}) custom-call(bf16[200,1024]{1,0:T(8,128)(2,1)} %bitcast.5, bf16[1024,1024]{1,0:T(8,128)(2,1)} %aint_hbm.1, bf16[1024,512]{1,0:T(8,128)(2,1)} %ahalo_hbm.1, s32[4,128]{1,0:T(4,128)} %idx_hbm.1, bf16[200,512]{1,0:T(8,128)(2,1)} %w0_hbm.1, ...), custom_call_target="tpu_custom_call" | custom-call | tf_op jit(solution)/shard_map/pallas_call | solution.py:350
  41.7 1.1 %shard_map.95 = (f32[200,512]{1,0:T(8,128)}, f32[107,512]{1,0:T(8,128)}, f32[200,1024]{1,0:T(8,128)}) custom-call(f32[200,512]{1,0:T(8,128)S(1)} %get-tuple-element.9.a, f32[107,512]{1,0:T(8,128)S(1)} %get-tuple-element.10.b, f32[200,1024]{1,0:T(8,128)S(1)} %get-tuple-element.11.c), custom_call_target="tpu_custom_call" | custom-call | tf_op jit(solution)/shard_map/pallas_call | solution.py:392

commit v4 on v3

--- a/solution.py
+++ b/solution.py
@@ -13,10 +13,13 @@
 SLOTS = 128
 ANY = pl.BlockSpec(memory_space=pl.ANY)
 VMEM = pl.BlockSpec(memory_space=pltpu.VMEM)
-STAGES = (
-    (("rs", "c"), ("rs", "zyx"), ("ag", "zyx"), ("ag", "c")),
-    (("rs", "zyc"), ("bc", "x"), ("ag", "zyc")),
+FULL = (("rs", "c"), ("rs", "zyx"), ("ag", "zyx"), ("ag", "c"))
+PLANE = (("rs", "zy"), ("bc", "xc"), ("ag", "zy"))
+SUMS = (
+    (1, 0, 4, FULL),
+    (2, 0, 4, PLANE),
 )
+ORDER = "WaEZbagbabdaba"
 AXES = "zyxc"
 
 
@@ -93,15 +96,15 @@
             return out
         return p, device
 
-    def each(self, size, body):
+    def each(self, size, body, first=1):
         if size <= 8:
-            for d in range(1, size):
+            for d in range(first, size):
                 body(d)
         else:
-            pl.loop(1, size)(body)
+            pl.loop(first, size)(body)
 
     def step(self):
-        next(self.steps, None)
+        return next(self.steps, False)
 
     def run(self, count):
         ar, res, rb = self.ar, self.res, self.rb
@@ -120,7 +123,7 @@
                         send_sem=send, recv_sem=recv, device_id={"nodes": device(to)})
                     when(None if full else to < owners, copy.start)
                 when(active, lambda: self.each(size, start))
-                yield
+                yield True
                 mine = both(active, None if full else p < owners)
                 new = first + p * piece
                 got = pl.ds(offset, slots)
@@ -152,7 +155,7 @@
                     self.each(size, start)
                     rb[pl.ds(offset + p * piece, piece)] = ar[mine]
                 when(active, spread)
-                yield
+                yield True
 
                 def collect():
                     wait_bytes(rb.at[pl.ds(offset, slots - piece)], recv)
@@ -163,12 +166,12 @@
             else:
                 mine = pl.ds(first, piece)
 
-                def start(d):
-                    pltpu.make_async_remote_copy(
+                def start(to):
+                    pl.when(to != p)(pltpu.make_async_remote_copy(
                         src_ref=res.at[mine], dst_ref=res.at[mine],
-                        send_sem=send, recv_sem=recv, device_id={"nodes": device(to_of(d))}).start()
-                when(active, lambda: self.each(size, start))
-                yield
+                        send_sem=send, recv_sem=recv, device_id={"nodes": device(to)}).start)
+                when(active, lambda: self.each(size, start, 0))
+                yield True
                 self.drains.append((active, send, (size - 1) * piece))
                 first, active, p, full = stack.pop()
                 if full:
@@ -184,8 +187,7 @@
 
 def kernel(n, xt_hbm, aint_hbm, ahalo_hbm, idx_hbm, w0_hbm, w1t_hbm, gt_hbm, dw1_ref, dw2t_ref, gft,
            xt, aint, ahalo, idx, w0, w1t, gt, st, s, e1t, o1, r1, g0, h0, zpart, d1t, z0t, h1t, g1, zh, z1part, z1t,
-           w0t, w1, gtp, ft, e0t, o0, r0, ar1, res1, rb1, ar2, res2, rb2,
-           load_sem, halo_send, halo_recv, send1, recv1, send2, recv2):
+           w0t, w1, gtp, ft, e0t, o0, r0, load_sem, halo_send, halo_recv, *sum_refs):
     dims = torus_dims(n)
     strides = tuple(dims[i + 1] * dims[i + 2] * dims[i + 3] if i == 0 else (dims[2] * dims[3], dims[3], 1)[i - 1] for i in range(4))
     me = lax.axis_index("nodes")
@@ -226,8 +228,10 @@
     halo_d1 = Halo(1, o1, r1, -1)
     halo_z = Halo(2, g1, zh, 1)
     halo_d0 = Halo(3, o0, r0, -1)
-    sum1 = Sum(me, pos, dims, strides, STAGES[0], ar1.shape[0], ar1, res1, rb1, send1, recv1)
-    sum2 = Sum(me, pos, dims, strides, STAGES[1], ar2.shape[0], ar2, res2, rb2, send2, recv2)
+    sums = []
+    for i, (_, _, _, stages) in enumerate(SUMS):
+        refs = sum_refs[5 * i:5 * i + 5]
+        sums.append(Sum(me, pos, dims, strides, stages, refs[0].shape[0], *refs))
 
     def put(ref, value):
         for k in range(4):
@@ -281,45 +285,48 @@
     d1 = d1t[...] + dot(take(r1), s[...])
     ft[...] = jnp.where(h1t[...] > 0, d1, 0.0).astype(BF)
 
-    def to_chunks(ref, value):
+    def to_chunks(which, value):
         groups = value.shape[0] // 8
-        for k in range(hidden // 128):
-            ref[k * groups:(k + 1) * groups] = value[:, k * 128:(k + 1) * 128].reshape(groups, 8, 128)
-
-    def from_chunks(out_ref, ref, rows):
-        groups = ref.shape[0] // (hidden // 128)
-        for k in range(hidden // 128):
-            out_ref[:, k * 128:(k + 1) * 128] = ref[k * groups:(k + 1) * groups].reshape(groups * 8, 128)[0:rows]
-
-    to_chunks(ar1, dot_nt(z0t[...], ft[...]))
-    sum1.step()
-    e0t[...] = dot(w0[...], ft[...]).astype(BF)
-    put(o0, dot(e0t[...], ahalo[...]))
-    halo_d0.start()
-
-    halo_z.wait_recv()
-    z1t[...] = (z1part[...] + dot_nt(hidden_of(take(zh)), ahalo[...])).astype(BF)
-    padded = -(-classes // 8) * 8
-    to_chunks(ar2, dot_nt(gtp[...], z1t[...])[0:padded])
-    sum2.step()
-
-    sum1.step()
-    gft[...] = dot(e0t[...], aint[...])
-    sum2.step()
-    sum1.step()
-    sum2.step()
-    halo_d0.wait_recv()
-    gft[...] = gft[...] + dot(take(r0), s[...])
-    for _ in range(3):
-        sum1.step()
-    from_chunks(dw1_ref, res1, feats)
-    for _ in range(3):
-        sum2.step()
-    from_chunks(dw2t_ref, res2, classes)
+        for (weight, lo, hi, _), total in zip(SUMS, sums):
+            if weight == which:
+                for k in range(lo, hi):
+                    total.ar[(k - lo) * groups:(k - lo + 1) * groups] = value[:, k * 128:(k + 1) * 128].reshape(groups, 8, 128)
+
+    def step(i):
+        weight, lo, hi, _ = SUMS[i]
+        if sums[i].step():
+            return
+        left.remove(i)
+        out_ref, rows = (dw1_ref, feats) if weight == 1 else (dw2t_ref, classes)
+        groups = sums[i].res.shape[0] // (hi - lo)
+        for k in range(lo, hi):
+            out_ref[:, k * 128:(k + 1) * 128] = sums[i].res[(k - lo) * groups:(k - lo + 1) * groups].reshape(groups * 8, 128)[0:rows]
+
+    left = list(range(len(SUMS)))
+    for event in ORDER:
+        if event == "W":
+            to_chunks(1, dot_nt(z0t[...], ft[...]))
+        elif event == "E":
+            e0t[...] = dot(w0[...], ft[...]).astype(BF)
+            put(o0, dot(e0t[...], ahalo[...]))
+            halo_d0.start()
+        elif event == "Z":
+            halo_z.wait_recv()
+            z1t[...] = (z1part[...] + dot_nt(hidden_of(take(zh)), ahalo[...])).astype(BF)
+            padded = -(-classes // 8) * 8
+            to_chunks(2, dot_nt(gtp[...], z1t[...])[0:padded])
+        elif event == "g":
+            gft[...] = dot(e0t[...], aint[...])
+        elif event == "d":
+            halo_d0.wait_recv()
+            gft[...] = gft[...] + dot(take(r0), s[...])
+        else:
+            step("abcABC".index(event))
+    assert not left
     for halo in (halo_x, halo_d1, halo_z, halo_d0):
         halo.wait_send()
-    sum1.drain()
-    sum2.drain()
+    for total in sums:
+        total.drain()
 
 
 def write_out(a, b, c, x, y, z, sem):
@@ -343,10 +350,12 @@
         slots = a_halo.shape[1]
         v = pltpu.VMEM
         dma = pltpu.SemaphoreType.DMA
-        counts = (feats // 8 * (hidden // 128), -(-classes // 8) * (hidden // 128))
-        sums = []
-        for stages, count in zip(STAGES, counts):
-            sums += [v((count, 8, 128), F32), v((count, 8, 128), F32), v((sum(p[5] for p in plan(dims, stages, count)), 8, 128), F32)]
+        groups = {1: feats // 8, 2: -(-classes // 8)}
+        sum_refs = []
+        for weight, lo, hi, stages in SUMS:
+            count = groups[weight] * (hi - lo)
+            received = sum(p[5] for p in plan(dims, stages, count))
+            sum_refs += [v((count, 8, 128), F32), v((count, 8, 128), F32), v((received, 8, 128), F32), dma((len(stages),)), dma((len(stages),))]
         outs = pl.pallas_call(
             functools.partial(kernel, n),
             out_shape=(v((feats, hidden), F32), v((classes, hidden), F32), v((feats, nodes), F32)),
@@ -382,9 +391,8 @@
                 v((feats, nodes), BF),
                 v((4, feats, SLOTS), BF),
                 v((4, feats, SLOTS), BF),
-                *sums,
                 dma((7,)), dma((4,)), dma((4,)),
-                dma((len(STAGES[0]),)), dma((len(STAGES[0]),)), dma((len(STAGES[1]),)), dma((len(STAGES[1]),)),
+                *sum_refs,
             ],
             compiler_params=pltpu.CompilerParams(collective_id=0, has_side_effects=True, vmem_limit_bytes=40 << 20),
         )(*[pltpu.with_memory_space_constraint(a, pltpu.HBM) for a in

time: 42.9 us -> 42 us (0.979)
  Pallas kernels: 42.2 us -> 41.3 us
    pallas_call x1, Pallas kernels: 41 us -> 40.2 us  [device_step(): pl.pallas_call(functools.partial(kernel, n), out_shape=(v((feats, hidden)...]
where the time goes in v4:
time: 42 us; the launch traced here: 41.9 us
  Pallas kernels  41.3 us (98%)
  between operations  0.64 us (2%)
    pallas_call x1, Pallas kernels, device_step(): pl.pallas_call(functools.partial(kernel, n), out_shape=(v((feats, hidden)...  40.2 us
    pallas_call x1, Pallas kernels, device_step(): pl.pallas_call(write_out, out_shape=tuple((jax.ShapeDtypeStruct(o.shape,...  1.13 us

profile of v4, /device:TPU:1, one launch (start us, length us, event | category | flops | bytes accessed | tf_op | source)
XLA Modules:
  0.0 41.9 jit_solution(131321973598367338)
XLA Ops:
  0.6 40.2 %shard_map.94 = (f32[200,512]{1,0:T(8,128)S(1)}, f32[107,512]{1,0:T(8,128)S(1)}, f32[200,1024]{1,0:T(8,128)S(1)}) custom-call(bf16[200,1024]{1,0:T(8,128)(2,1)} %bitcast.5, bf16[1024,1024]{1,0:T(8,128)(2,1)} %aint_hbm.1, bf16[1024,512]{1,0:T(8,128)(2,1)} %ahalo_hbm.1, s32[4,128]{1,0:T(4,128)} %idx_hbm.1, bf16[200,512]{1,0:T(8,128)(2,1)} %w0_hbm.1, ...), custom_call_target="tpu_custom_call" | custom-call | tf_op jit(solution)/shard_map/pallas_call | solution.py:359
  40.8 1.1 %shard_map.95 = (f32[200,512]{1,0:T(8,128)}, f32[107,512]{1,0:T(8,128)}, f32[200,1024]{1,0:T(8,128)}) custom-call(f32[200,512]{1,0:T(8,128)S(1)} %get-tuple-element.9.a, f32[107,512]{1,0:T(8,128)S(1)} %get-tuple-element.10.b, f32[200,1024]{1,0:T(8,128)S(1)} %get-tuple-element.11.c), custom_call_target="tpu_custom_call" | custom-call | tf_op jit(solution)/shard_map/pallas_call | solution.py:400

commit v5 on v4

--- a/solution.py
+++ b/solution.py
@@ -10,6 +10,8 @@
 BF = jnp.bfloat16
 F32 = jnp.float32
 OFFSETS = (1, -1, 2, -2)
+BLOCKS = (0, 2, 1, 3)
+ISSUE = (0, 2, 1, 3)
 SLOTS = 128
 ANY = pl.BlockSpec(memory_space=pl.ANY)
 VMEM = pl.BlockSpec(memory_space=pltpu.VMEM)
@@ -19,7 +21,7 @@
     (1, 0, 4, FULL),
     (2, 0, 4, PLANE),
 )
-ORDER = "WaEZbagbabdaba"
+ORDER = "WaEZbagbabdaab"
 AXES = "zyxc"
 
 
@@ -94,7 +96,33 @@
                 out = out + lax.rem(q, self.dims[a]) * self.strides[a]
                 q = lax.div(q, self.dims[a])
             return out
-        return p, device
+        def partner(i):
+            to, radix = 0, 1
+            for a in reversed(ids):
+                d = self.dims[a]
+                to = to + lax.rem(self.pos[a] + lax.rem(i, d) + 1, d) * radix
+                i, radix = lax.div(i, d), radix * d
+            return to
+
+        own = 0
+        for a in ids:
+            own = own * self.dims[a] + (self.dims[a] - 1)
+        return p, device, partner, own
+
+    def others(self, size, own, body):
+        if size <= 8:
+            for i in range(size):
+                if i != own:
+                    body(jnp.int32(i), i - (i > own))
+            return
+
+        @pl.loop(0, own)
+        def _(i):
+            body(i, i)
+
+        @pl.loop(own + 1, size)
+        def _(i):
+            body(i, i - 1)
 
     def each(self, size, body, first=1):
         if size <= 8:
@@ -110,19 +138,19 @@
         ar, res, rb = self.ar, self.res, self.rb
         first, active, offset, stack = 0, None, 0, []
         for i, (kind, axes, size, owners, piece, slots) in enumerate(self.plan):
-            p, device = self.group(axes)
+            p, device, partner, own = self.group(axes)
             send, recv = self.send_sem.at[i], self.recv_sem.at[i]
             to_of = lambda d: lax.rem(p + d, size)
             if kind == "rs":
                 full = owners == size
 
-                def start(d):
-                    to = to_of(d)
+                def start(i, slot):
+                    to = partner(i)
                     copy = pltpu.make_async_remote_copy(
-                        src_ref=ar.at[pl.ds(first + to * piece, piece)], dst_ref=rb.at[pl.ds(offset + (d - 1) * piece, piece)],
+                        src_ref=ar.at[pl.ds(first + to * piece, piece)], dst_ref=rb.at[pl.ds(offset + slot * piece, piece)],
                         send_sem=send, recv_sem=recv, device_id={"nodes": device(to)})
                     when(None if full else to < owners, copy.start)
-                when(active, lambda: self.each(size, start))
+                when(active, lambda: self.others(size, own, start))
                 yield True
                 mine = both(active, None if full else p < owners)
                 new = first + p * piece
@@ -165,14 +193,24 @@
                 offset += slots
             else:
                 mine = pl.ds(first, piece)
+                ahead = axes == "zyx" and i + 1 < len(self.plan) and self.plan[i + 1][1] == "c"
+                if axes == "c":
+                    active = both(active, self.me >= 2)
 
                 def start(to):
                     pl.when(to != p)(pltpu.make_async_remote_copy(
                         src_ref=res.at[mine], dst_ref=res.at[mine],
                         send_sem=send, recv_sem=recv, device_id={"nodes": device(to)}).start)
-                when(active, lambda: self.each(size, start, 0))
+
+                def spread():
+                    if ahead:
+                        pltpu.make_async_remote_copy(
+                            src_ref=res.at[mine], dst_ref=res.at[mine],
+                            send_sem=send, recv_sem=self.recv_sem.at[i + 1], device_id={"nodes": 1 - self.pos[3]}).start()
+                    self.each(size, start, 0)
+                when(active, spread)
                 yield True
-                self.drains.append((active, send, (size - 1) * piece))
+                self.drains.append((active, send, (size - 1 + ahead) * piece))
                 first, active, p, full = stack.pop()
                 if full:
                     when(active, lambda: wait_bytes(res.at[pl.ds(0, (size - 1) * piece)], recv))
@@ -202,24 +240,34 @@
         pl.semaphore_signal(barrier, inc=1, device_id={"nodes": lax.rem(me + i, n)})
 
     loads = [pltpu.make_async_copy(src, dst, load_sem.at[i]) for i, (src, dst) in enumerate([
-        (idx_hbm, idx), (xt_hbm, xt), (w1t_hbm, w1t), (gt_hbm, gt), (ahalo_hbm, ahalo), (aint_hbm, aint), (w0_hbm, w0)])]
-    for load in loads:
+        (idx_hbm, idx), (xt_hbm, xt), (w1t_hbm, w1t), (gt_hbm, gt), (aint_hbm, aint), (w0_hbm, w0)])]
+    for load in loads[:4]:
         load.start()
+    for c, k in enumerate(BLOCKS):
+        pltpu.make_async_copy(
+            ahalo_hbm.at[:, pl.ds(k * SLOTS, SLOTS)], ahalo.at[c // 2, :, pl.ds(c % 2 * SLOTS, SLOTS)], load_sem.at[6]).start()
+    for load in loads[4:]:
+        load.start()
+
+    ahead = lax.div(pos[2], dims[2] // 2)
+    behind = 1 - ahead
 
     class Halo:
         def __init__(self, which, src, dst, sign):
             self.src, self.dst = src, dst
-            self.send, self.recv = halo_send.at[which], halo_recv.at[which]
-            self.sign = sign
+            self.send, self.recv = halo_send.at[which], [halo_recv.at[2 * which], halo_recv.at[2 * which + 1]]
+            self.which, self.sign = which, sign
+            self.first, self.second = (behind, ahead) if sign > 0 else (ahead, behind)
 
         def start(self):
-            for k, o in enumerate(OFFSETS):
+            for c in ISSUE:
+                o = OFFSETS[BLOCKS[c]]
                 pltpu.make_async_remote_copy(
-                    src_ref=self.src.at[k], dst_ref=self.dst.at[k], send_sem=self.send, recv_sem=self.recv,
+                    src_ref=self.src.at[c // 2, c % 2], dst_ref=self.dst.at[c // 2, c % 2], send_sem=self.send, recv_sem=self.recv[c // 2],
                     device_id={"nodes": lax.rem(me + self.sign * o + n, n)}).start()
 
-        def wait_recv(self):
-            wait_bytes(self.dst, self.recv)
+        def wait_recv(self, half):
+            wait_bytes(self.dst.at[half], halo_recv.at[2 * self.which + half])
 
         def wait_send(self):
             wait_bytes(self.src, self.send)
@@ -234,17 +282,23 @@
         sums.append(Sum(me, pos, dims, strides, stages, refs[0].shape[0], *refs))
 
     def put(ref, value):
-        for k in range(4):
-            ref[k] = value[:, k * SLOTS:(k + 1) * SLOTS].astype(BF)
-
-    def take(ref):
-        return jnp.concatenate([ref[k] for k in range(4)], axis=1)
+        for c in range(4):
+            ref[c // 2, c % 2] = value[:, c * SLOTS:(c + 1) * SLOTS].astype(BF)
+
+    def take(ref, half):
+        return jnp.concatenate([ref[half, 0], ref[half, 1]], axis=1)
+
+    def outward(rows):
+        return jnp.concatenate([dot(rows, ahalo[0]), dot(rows, ahalo[1])], axis=1)
+
+    def half_rows(half):
+        return s[pl.ds(pl.multiple_of(half * 2 * SLOTS, 2 * SLOTS), 2 * SLOTS)]
 
     loads[0].wait()
     sub = lax.broadcasted_iota(jnp.int32, (nodes, SLOTS), 0)
-    for k in range(4):
+    for c, k in enumerate(BLOCKS):
         row = jnp.broadcast_to(idx[k:k + 1, :], (nodes, SLOTS))
-        st[:, k * SLOTS:(k + 1) * SLOTS] = jnp.where(row == sub, 1.0, 0.0).astype(BF)
+        st[:, c * SLOTS:(c + 1) * SLOTS] = jnp.where(row == sub, 1.0, 0.0).astype(BF)
 
     loads[1].wait()
     put(g0, dot(xt[...], st[...]))
@@ -253,36 +307,40 @@
     w1[...] = jnp.concatenate([w1t[...].astype(F32), jnp.zeros((128 - classes, hidden), F32)], axis=0).T.astype(BF)
     gtp[...] = jnp.concatenate([gt[...].astype(F32), jnp.zeros((128 - classes, nodes), F32)], axis=0).astype(BF)
     e1t[...] = dot(w1[...], gtp[...]).astype(BF)
-    loads[4].wait()
-    put(o1, dot(e1t[...], ahalo[...]))
+    wait_bytes(ahalo, load_sem.at[6])
+    put(o1, outward(e1t[...]))
 
     pl.semaphore_wait(barrier, n - 1)
     halo_x.start()
 
+    loads[4].wait()
     loads[5].wait()
-    loads[6].wait()
     zpart[...] = dot_nt(xt[...], aint[...])
     halo_d1.start()
     w0t[...] = w0[...].astype(F32).T.astype(BF)
     lane = lax.broadcasted_iota(jnp.int32, (SLOTS, SLOTS), 1)
-    for k in range(4):
+    for c, k in enumerate(BLOCKS):
         col = jnp.broadcast_to(idx[k:k + 1, :], (SLOTS, SLOTS)).T
         for b in range(nodes // SLOTS):
-            s[k * SLOTS:(k + 1) * SLOTS, b * SLOTS:(b + 1) * SLOTS] = jnp.where(col == lane + b * SLOTS, 1.0, 0.0).astype(BF)
+            s[c * SLOTS:(c + 1) * SLOTS, b * SLOTS:(b + 1) * SLOTS] = jnp.where(col == lane + b * SLOTS, 1.0, 0.0).astype(BF)
     d1t[...] = dot(e1t[...], aint[...])
 
     def hidden_of(zt):
         return jnp.maximum(dot(w0t[...], zt), 0.0).astype(BF)
 
-    halo_x.wait_recv()
-    z0t[...] = (zpart[...] + dot_nt(take(h0), ahalo[...])).astype(BF)
+    halo_x.wait_recv(halo_x.first)
+    zpart[...] = zpart[...] + dot_nt(take(h0, halo_x.first), ahalo[halo_x.first])
+    halo_x.wait_recv(halo_x.second)
+    z0t[...] = (zpart[...] + dot_nt(take(h0, halo_x.second), ahalo[halo_x.second])).astype(BF)
     put(g1, dot(z0t[...], st[...]))
     halo_z.start()
     h1t[...] = hidden_of(z0t[...])
     z1part[...] = dot_nt(h1t[...], aint[...])
 
-    halo_d1.wait_recv()
-    d1 = d1t[...] + dot(take(r1), s[...])
+    halo_d1.wait_recv(halo_d1.first)
+    d1t[...] = d1t[...] + dot(take(r1, halo_d1.first), half_rows(halo_d1.first))
+    halo_d1.wait_recv(halo_d1.second)
+    d1 = d1t[...] + dot(take(r1, halo_d1.second), half_rows(halo_d1.second))
     ft[...] = jnp.where(h1t[...] > 0, d1, 0.0).astype(BF)
 
     def to_chunks(which, value):
@@ -308,18 +366,21 @@
             to_chunks(1, dot_nt(z0t[...], ft[...]))
         elif event == "E":
             e0t[...] = dot(w0[...], ft[...]).astype(BF)
-            put(o0, dot(e0t[...], ahalo[...]))
+            put(o0, outward(e0t[...]))
             halo_d0.start()
         elif event == "Z":
-            halo_z.wait_recv()
-            z1t[...] = (z1part[...] + dot_nt(hidden_of(take(zh)), ahalo[...])).astype(BF)
+            halo_z.wait_recv(halo_z.first)
+            z1part[...] = z1part[...] + dot_nt(hidden_of(take(zh, halo_z.first)), ahalo[halo_z.first])
+            halo_z.wait_recv(halo_z.second)
+            z1t[...] = (z1part[...] + dot_nt(hidden_of(take(zh, halo_z.second)), ahalo[halo_z.second])).astype(BF)
             padded = -(-classes // 8) * 8
             to_chunks(2, dot_nt(gtp[...], z1t[...])[0:padded])
         elif event == "g":
             gft[...] = dot(e0t[...], aint[...])
         elif event == "d":
-            halo_d0.wait_recv()
-            gft[...] = gft[...] + dot(take(r0), s[...])
+            for half in range(2):
+                halo_d0.wait_recv(half)
+                gft[...] = gft[...] + dot(take(r0, half), half_rows(half))
         else:
             step("abcABC".index(event))
     assert not left
@@ -364,7 +425,7 @@
             scratch_shapes=[
                 v((feats, nodes), BF),
                 v((nodes, nodes), BF),
-                v((nodes, slots), BF),
+                v((2, nodes, slots // 2), BF),
                 v((4, SLOTS), jnp.int32),
                 v((feats, hidden), BF),
                 v((classes, hidden), BF),
@@ -372,16 +433,16 @@
                 v((nodes, slots), BF),
                 v((slots, nodes), BF),
                 v((hidden, nodes), BF),
-                v((4, hidden, SLOTS), BF),
-                v((4, hidden, SLOTS), BF),
-                v((4, feats, SLOTS), BF),
-                v((4, feats, SLOTS), BF),
+                v((2, 2, hidden, SLOTS), BF),
+                v((2, 2, hidden, SLOTS), BF),
+                v((2, 2, feats, SLOTS), BF),
+                v((2, 2, feats, SLOTS), BF),
                 v((feats, nodes), F32),
                 v((hidden, nodes), F32),
                 v((feats, nodes), BF),
                 v((hidden, nodes), BF),
-                v((4, feats, SLOTS), BF),
-                v((4, feats, SLOTS), BF),
+                v((2, 2, feats, SLOTS), BF),
+                v((2, 2, feats, SLOTS), BF),
                 v((hidden, nodes), F32),
                 v((hidden, nodes), BF),
                 v((hidden, feats), BF),
@@ -389,9 +450,9 @@
                 v((128, nodes), BF),
                 v((hidden, nodes), BF),
                 v((feats, nodes), BF),
-                v((4, feats, SLOTS), BF),
-                v((4, feats, SLOTS), BF),
-                dma((7,)), dma((4,)), dma((4,)),
+                v((2, 2, feats, SLOTS), BF),
+                v((2, 2, feats, SLOTS), BF),
+                dma((7,)), dma((4,)), dma((8,)),
                 *sum_refs,
             ],
             compiler_params=pltpu.CompilerParams(collective_id=0, has_side_effects=True, vmem_limit_bytes=40 << 20),

time: 42 us -> 41.1 us (0.979); the launches traced: 41.9 us -> 40.4 us
  Pallas kernels: 41.3 us -> 39.8 us
    pallas_call x1, Pallas kernels: 40.2 us -> 38.7 us  [device_step(): pl.pallas_call(functools.partial(kernel, n), out_shape=(v((feats, hidden)...]
where the time goes in v5:
time: 41.1 us; the launch traced here: 40.4 us
  Pallas kernels  39.8 us (97%)
  between operations  0.64 us (2%)
    pallas_call x1, Pallas kernels, device_step(): pl.pallas_call(functools.partial(kernel, n), out_shape=(v((feats, hidden)...  38.7 us
    pallas_call x1, Pallas kernels, device_step(): pl.pallas_call(write_out, out_shape=tuple((jax.ShapeDtypeStruct(o.shape,...  1.13 us

profile of v5, /device:TPU:1, one launch (start us, length us, event | category | flops | bytes accessed | tf_op | source)
XLA Modules:
  0.0 40.4 jit_solution(3315737688210990304)
XLA Ops:
  0.6 38.7 %shard_map.94 = (f32[200,512]{1,0:T(8,128)S(1)}, f32[107,512]{1,0:T(8,128)S(1)}, f32[200,1024]{1,0:T(8,128)S(1)}) custom-call(bf16[200,1024]{1,0:T(8,128)(2,1)} %bitcast.5, bf16[1024,1024]{1,0:T(8,128)(2,1)} %aint_hbm.1, bf16[1024,512]{1,0:T(8,128)(2,1)} %ahalo_hbm.1, s32[4,128]{1,0:T(4,128)} %idx_hbm.1, bf16[200,512]{1,0:T(8,128)(2,1)} %w0_hbm.1, ...), custom_call_target="tpu_custom_call" | custom-call | tf_op jit(solution)/shard_map/pallas_call | solution.py:420
  39.3 1.1 %shard_map.95 = (f32[200,512]{1,0:T(8,128)}, f32[107,512]{1,0:T(8,128)}, f32[200,1024]{1,0:T(8,128)}) custom-call(f32[200,512]{1,0:T(8,128)S(1)} %get-tuple-element.9.a, f32[107,512]{1,0:T(8,128)S(1)} %get-tuple-element.10.b, f32[200,1024]{1,0:T(8,128)S(1)} %get-tuple-element.11.c), custom_call_target="tpu_custom_call" | custom-call | tf_op jit(solution)/shard_map/pallas_call | solution.py:461

commit v6 on v5

--- a/solution.py
+++ b/solution.py
@@ -235,9 +235,11 @@
 
     barrier = pltpu.get_barrier_semaphore()
 
-    @pl.loop(1, n)
-    def _(i):
+    def greet(i):
         pl.semaphore_signal(barrier, inc=1, device_id={"nodes": lax.rem(me + i, n)})
+
+    for i in (1, 2, n - 2, n - 1):
+        greet(i)
 
     loads = [pltpu.make_async_copy(src, dst, load_sem.at[i]) for i, (src, dst) in enumerate([
         (idx_hbm, idx), (xt_hbm, xt), (w1t_hbm, w1t), (gt_hbm, gt), (aint_hbm, aint), (w0_hbm, w0)])]
@@ -248,6 +250,7 @@
             ahalo_hbm.at[:, pl.ds(k * SLOTS, SLOTS)], ahalo.at[c // 2, :, pl.ds(c % 2 * SLOTS, SLOTS)], load_sem.at[6]).start()
     for load in loads[4:]:
         load.start()
+    pl.loop(3, n - 2)(greet)
 
     ahead = lax.div(pos[2], dims[2] // 2)
     behind = 1 - ahead

time: 41.1 us -> 40.8 us (level); the launches traced: 40.4 us -> 40.6 us
  no operation moved by 1% of the time
where the time goes in v6:
time: 40.8 us; the launch traced here: 40.6 us
  Pallas kernels  40 us (98%)
  between operations  0.64 us (2%)
    pallas_call x1, Pallas kernels, device_step(): pl.pallas_call(functools.partial(kernel, n), out_shape=(v((feats, hidden)...  38.9 us
    pallas_call x1, Pallas kernels, device_step(): pl.pallas_call(write_out, out_shape=tuple((jax.ShapeDtypeStruct(o.shape,...  1.13 us

profile of v6, /device:TPU:1, one launch (start us, length us, event | category | flops | bytes accessed | tf_op | source)
XLA Modules:
  0.0 40.6 jit_solution(18204993262090589101)
XLA Ops:
  0.6 38.9 %shard_map.94 = (f32[200,512]{1,0:T(8,128)S(1)}, f32[107,512]{1,0:T(8,128)S(1)}, f32[200,1024]{1,0:T(8,128)S(1)}) custom-call(bf16[200,1024]{1,0:T(8,128)(2,1)} %bitcast.5, bf16[1024,1024]{1,0:T(8,128)(2,1)} %aint_hbm.1, bf16[1024,512]{1,0:T(8,128)(2,1)} %ahalo_hbm.1, s32[4,128]{1,0:T(4,128)} %idx_hbm.1, bf16[200,512]{1,0:T(8,128)(2,1)} %w0_hbm.1, ...), custom_call_target="tpu_custom_call" | custom-call | tf_op jit(solution)/shard_map/pallas_call | solution.py:423
  39.5 1.1 %shard_map.95 = (f32[200,512]{1,0:T(8,128)}, f32[107,512]{1,0:T(8,128)}, f32[200,1024]{1,0:T(8,128)}) custom-call(f32[200,512]{1,0:T(8,128)S(1)} %get-tuple-element.9.a, f32[107,512]{1,0:T(8,128)S(1)} %get-tuple-element.10.b, f32[200,1024]{1,0:T(8,128)S(1)} %get-tuple-element.11.c), custom_call_target="tpu_custom_call" | custom-call | tf_op jit(solution)/shard_map/pallas_call | solution.py:464

commit v7 on v6

--- a/solution.py
+++ b/solution.py
@@ -238,8 +238,6 @@
     def greet(i):
         pl.semaphore_signal(barrier, inc=1, device_id={"nodes": lax.rem(me + i, n)})
 
-    for i in (1, 2, n - 2, n - 1):
-        greet(i)
 
     loads = [pltpu.make_async_copy(src, dst, load_sem.at[i]) for i, (src, dst) in enumerate([
         (idx_hbm, idx), (xt_hbm, xt), (w1t_hbm, w1t), (gt_hbm, gt), (aint_hbm, aint), (w0_hbm, w0)])]
@@ -250,6 +248,8 @@
             ahalo_hbm.at[:, pl.ds(k * SLOTS, SLOTS)], ahalo.at[c // 2, :, pl.ds(c % 2 * SLOTS, SLOTS)], load_sem.at[6]).start()
     for load in loads[4:]:
         load.start()
+    for i in (1, 2, n - 2, n - 1):
+        greet(i)
     pl.loop(3, n - 2)(greet)
 
     ahead = lax.div(pos[2], dims[2] // 2)

time: 40.8 us -> 40.6 us (level)
  no operation moved by 1% of the time
where the time goes in v7:
time: 40.6 us; the launch traced here: 40.5 us
  Pallas kernels  39.8 us (98%)
  between operations  0.64 us (2%)
    pallas_call x1, Pallas kernels, device_step(): pl.pallas_call(functools.partial(kernel, n), out_shape=(v((feats, hidden)...  38.7 us
    pallas_call x1, Pallas kernels, device_step(): pl.pallas_call(write_out, out_shape=tuple((jax.ShapeDtypeStruct(o.shape,...  1.13 us

profile of v7, /device:TPU:1, one launch (start us, length us, event | category | flops | bytes accessed | tf_op | source)
XLA Modules:
  0.0 40.5 jit_solution(15761467575958491041)
XLA Ops:
  0.6 38.7 %shard_map.94 = (f32[200,512]{1,0:T(8,128)S(1)}, f32[107,512]{1,0:T(8,128)S(1)}, f32[200,1024]{1,0:T(8,128)S(1)}) custom-call(bf16[200,1024]{1,0:T(8,128)(2,1)} %bitcast.5, bf16[1024,1024]{1,0:T(8,128)(2,1)} %aint_hbm.1, bf16[1024,512]{1,0:T(8,128)(2,1)} %ahalo_hbm.1, s32[4,128]{1,0:T(4,128)} %idx_hbm.1, bf16[200,512]{1,0:T(8,128)(2,1)} %w0_hbm.1, ...), custom_call_target="tpu_custom_call" | custom-call | tf_op jit(solution)/shard_map/pallas_call | solution.py:423
  39.3 1.1 %shard_map.95 = (f32[200,512]{1,0:T(8,128)}, f32[107,512]{1,0:T(8,128)}, f32[200,1024]{1,0:T(8,128)}) custom-call(f32[200,512]{1,0:T(8,128)S(1)} %get-tuple-element.9.a, f32[107,512]{1,0:T(8,128)S(1)} %get-tuple-element.10.b, f32[200,1024]{1,0:T(8,128)S(1)} %get-tuple-element.11.c), custom_call_target="tpu_custom_call" | custom-call | tf_op jit(solution)/shard_map/pallas_call | solution.py:464

commit v8 on v7

--- a/solution.py
+++ b/solution.py
@@ -21,7 +21,7 @@
     (1, 0, 4, FULL),
     (2, 0, 4, PLANE),
 )
-ORDER = "WaEZbagbabdaab"
+ORDER = "WaEZbabgabdaab"
 AXES = "zyxc"
 
 

time: 40.6 us -> 41.2 us (1.015)
  Pallas kernels: 39.8 us -> 40.5 us
    pallas_call x1, Pallas kernels: 38.7 us -> 39.4 us  [device_step(): pl.pallas_call(functools.partial(kernel, n), out_shape=(v((feats, hidden)...]
where the time goes in v8:
time: 41.2 us; the launch traced here: 41.1 us
  Pallas kernels  40.5 us (98%)
  between operations  0.64 us (2%)
    pallas_call x1, Pallas kernels, device_step(): pl.pallas_call(functools.partial(kernel, n), out_shape=(v((feats, hidden)...  39.4 us
    pallas_call x1, Pallas kernels, device_step(): pl.pallas_call(write_out, out_shape=tuple((jax.ShapeDtypeStruct(o.shape,...  1.13 us

profile of v8, /device:TPU:1, one launch (start us, length us, event | category | flops | bytes accessed | tf_op | source)
XLA Modules:
  0.0 41.1 jit_solution(18120974388287065607)
XLA Ops:
  0.6 39.4 %shard_map.94 = (f32[200,512]{1,0:T(8,128)S(1)}, f32[107,512]{1,0:T(8,128)S(1)}, f32[200,1024]{1,0:T(8,128)S(1)}) custom-call(bf16[200,1024]{1,0:T(8,128)(2,1)} %bitcast.5, bf16[1024,1024]{1,0:T(8,128)(2,1)} %aint_hbm.1, bf16[1024,512]{1,0:T(8,128)(2,1)} %ahalo_hbm.1, s32[4,128]{1,0:T(4,128)} %idx_hbm.1, bf16[200,512]{1,0:T(8,128)(2,1)} %w0_hbm.1, ...), custom_call_target="tpu_custom_call" | custom-call | tf_op jit(solution)/shard_map/pallas_call | solution.py:423
  40.0 1.1 %shard_map.95 = (f32[200,512]{1,0:T(8,128)}, f32[107,512]{1,0:T(8,128)}, f32[200,1024]{1,0:T(8,128)}) custom-call(f32[200,512]{1,0:T(8,128)S(1)} %get-tuple-element.9.a, f32[107,512]{1,0:T(8,128)S(1)} %get-tuple-element.10.b, f32[200,1024]{1,0:T(8,128)S(1)} %get-tuple-element.11.c), custom_call_target="tpu_custom_call" | custom-call | tf_op jit(solution)/shard_map/pallas_call | solution.py:464
